TPU v7x, 256 devices: a whole 4x4x8 slice. The times are simulated.
256 devices in a mesh: section: 8 (over x, core), expert: 32 (over z, y).
Axes of the slice: x: 4, y: 4, z: 8, core: 2. Of those that a mesh axis runs over, the one named last changes fastest.
Arguments:
- tokens: bfloat16 [4, 1024, 2048], P(None, 'expert'), may hold values from -6 to 6
- attn_norm: float32 [8, 2048], P('section'), may hold values from 0.5 to 2
- moe_norm: float32 [8, 2048], P('section'), may hold values from 0.5 to 2
- query_weight: bfloat16 [8, 2048, 1024], P('section', 'expert'), may hold values from -4 to 4
- key_weight: bfloat16 [8, 2048, 128], P('section', 'expert'), may hold values from -0.125 to 0.125
- value_weight: bfloat16 [8, 2048, 128], P('section', 'expert'), may hold values from -0.125 to 0.125
- out_weight: bfloat16 [8, 1024, 2048], P('section', 'expert'), may hold values from -0.1875 to 0.1875
- gate_proj: bfloat16 [8, 32, 2048, 704], P('section', 'expert'), may hold values from -0.125 to 0.125
- up_proj: bfloat16 [8, 32, 2048, 704], P('section', 'expert'), may hold values from -0.125 to 0.125
- down_proj: bfloat16 [8, 32, 704, 2048], P('section', 'expert'), may hold values from -0.21875 to 0.21875
- routes: int32 [8, 4, 1024, 6], P('section', None, 'expert'), may hold values from 0 to 31, all different within a row; in each aligned block of 32 rows (0 to 31, 32 to 63, ..., all dimensions but the last counted through in order) at most 8 rows name the same one
- weights_code: int32 [8, 4, 1024, 6], P('section', None, 'expert'), may hold values from 8 to 64
Outputs:
- hidden_states: bfloat16 [8, 4, 1024, 2048], P('section', None, 'expert')
Inputs may be any that keep to these rules, and one draw needn't show every extreme that they name: `routes`: each row names 6 different experts. In each aligned block of 32 rows (one sequence's tokens of one micro-batch of one layer) no expert is named by more than 8 rows, a bound that some block reaches.
All inputs are finite; a program needn't handle non-finite values.
Results may differ from a plain program's by a relative error of at most 0.03.
Values may be sent and summed in bfloat16 or wider, within the bound.
No kernel may reach another device: no remote copies, remote signals or barrier semaphores. Data moves between devices by JAX's collectives and lax.ppermute only.
A program may use at most 128 MiB of HBM per device.

v0:
```python
import jax
import jax.numpy as jnp
from jax import lax
from jax.sharding import PartitionSpec as P

epsilon = 1e-06


def shifted(value, axis, steps):
    count = lax.axis_size(axis)
    initial, last = (max(0, -steps), min(count, count - steps))
    return lax.ppermute(value, axis, [(source, source + steps) for source in range(initial, last)])


def rms_scale(features, gain_vector):
    return (
        features
        * lax.rsqrt(jnp.mean(features * features, axis=-1, keepdims=True) + epsilon)
        * gain_vector
    )


def expert_rows(slot_rows, gate_matrix, up_matrix, down_matrix):
    gated = jnp.dot(slot_rows, gate_matrix, preferred_element_type=jnp.float32)
    lifted = jnp.dot(slot_rows, up_matrix, preferred_element_type=jnp.float32)
    hidden = (jax.nn.silu(gated) * lifted).astype(jnp.bfloat16)
    return jnp.dot(hidden, down_matrix, preferred_element_type=jnp.float32).astype(jnp.bfloat16)


def route_tables(picks_block, codes_block, expert_count, capacity):
    tok_rows, pick_count = picks_block.shape
    flat_ids = picks_block.reshape(-1)
    matches = (flat_ids[:, None] == jnp.arange(expert_count, dtype=jnp.int32)[None, :]).astype(
        jnp.int32
    )
    slot_ranks = jnp.sum((jnp.cumsum(matches, axis=0) - matches) * matches, axis=1)
    columns = flat_ids * capacity + slot_ranks
    onehot = (
        columns[:, None] == jnp.arange(expert_count * capacity, dtype=jnp.int32)[None, :]
    ).astype(jnp.float32)
    onehot = onehot.reshape(tok_rows, pick_count, expert_count * capacity)
    scatter_table = jnp.sum(onehot, axis=1).astype(jnp.bfloat16)
    pick_weights = codes_block.astype(jnp.float32) / 64.0
    combine_table = jnp.sum(onehot * pick_weights[:, :, None], axis=1).astype(jnp.bfloat16)
    return (scatter_table, combine_table)


def shards(
    tokens,
    attn_norm,
    moe_norm,
    query_weight,
    key_weight,
    value_weight,
    out_weight,
    gate_proj,
    up_proj,
    down_proj,
    routes,
    weights_code,
):
    section_count = lax.axis_size("section")
    section_index = lax.axis_index("section")
    expert_devices = lax.axis_size("expert")
    micro_count, tok_rows, model_width = tokens.shape
    pick_count = routes.shape[3]
    expert_count = expert_devices * gate_proj.shape[1]
    capacity = min(tok_rows, tok_rows * pick_count * 4 // (3 * expert_count))
    full_query, full_key, full_value, full_out = (
        lax.all_gather(query_weight, "expert", axis=1, tiled=True),
        lax.all_gather(key_weight, "expert", axis=1, tiled=True),
        lax.all_gather(value_weight, "expert", axis=1, tiled=True),
        lax.all_gather(out_weight, "expert", axis=1, tiled=True),
    )
    full_query = full_query[0]
    full_key = full_key[0]
    full_value = full_value[0]
    full_out = full_out[0]
    head_size = full_key.shape[-1]
    head_count = full_query.shape[-1] // head_size
    length = micro_count * tok_rows
    score_scale = head_size ** (-0.5)
    attn_gain = attn_norm[0]
    moe_gain = moe_norm[0]
    gate_matrix = gate_proj[0, 0]
    up_matrix = up_proj[0, 0]
    down_matrix = down_proj[0, 0]
    route_layer = routes[0]
    code_layer = weights_code[0]

    def feed_rows(slot_rows):
        return expert_rows(slot_rows, gate_matrix, up_matrix, down_matrix)

    def blank_rows(slot_rows):
        return jnp.zeros((slot_rows.shape[0], model_width), jnp.bfloat16)

    def advance(tick_index, state_carry):
        inbound, key_cache, value_cache, stored = state_carry
        block_index = tick_index - section_index
        active = (block_index >= 0) & (block_index < micro_count)
        clipped = jnp.clip(block_index, 0, micro_count - 1)
        first_rows = lax.dynamic_index_in_dim(tokens, clipped, 0, keepdims=False)
        layer_input = jnp.where(section_index == 0, first_rows, inbound)
        picks_block = lax.dynamic_index_in_dim(route_layer, clipped, 0, keepdims=False)
        codes_block = lax.dynamic_index_in_dim(code_layer, clipped, 0, keepdims=False)
        scatter_table, combine_table = route_tables(
            picks_block, codes_block, expert_count, capacity
        )
        wide_input = layer_input.astype(jnp.float32)
        moe_input = rms_scale(wide_input, moe_gain).astype(jnp.bfloat16)

        def attend(caches):
            old_keys, old_values = caches
            normed = rms_scale(wide_input, attn_gain).astype(jnp.bfloat16)
            query_rows = jnp.dot(normed, full_query, preferred_element_type=jnp.float32).astype(
                jnp.bfloat16
            )
            query_rows = query_rows.reshape(tok_rows, head_count, head_size)
            new_keys = jnp.dot(normed, full_key, preferred_element_type=jnp.float32).astype(
                jnp.bfloat16
            )
            new_values = jnp.dot(normed, full_value, preferred_element_type=jnp.float32).astype(
                jnp.bfloat16
            )
            offset = clipped * tok_rows
            key_vectors = lax.dynamic_update_slice_in_dim(old_keys, new_keys, offset, 0)
            value_vectors = lax.dynamic_update_slice_in_dim(old_values, new_values, offset, 0)
            attention_scores = (
                jnp.einsum(
                    "qhd,kd->hqk", query_rows, key_vectors, preferred_element_type=jnp.float32
                )
                * score_scale
            )
            positions = offset + jnp.arange(tok_rows, dtype=jnp.int32)
            causal = jnp.arange(length, dtype=jnp.int32)[None, :] <= positions[:, None]
            attention_scores = jnp.where(causal[None], attention_scores, -1e30)
            highest = jnp.max(attention_scores, axis=-1, keepdims=True)
            exponent = jnp.exp(attention_scores - highest)
            attention_probabilities = (exponent / jnp.sum(exponent, axis=-1, keepdims=True)).astype(
                jnp.bfloat16
            )
            attended_values = jnp.einsum(
                "hqk,kd->qhd",
                attention_probabilities,
                value_vectors,
                preferred_element_type=jnp.float32,
            )
            attended_values = attended_values.astype(jnp.bfloat16).reshape(
                tok_rows, head_count * head_size
            )
            attended = jnp.dot(attended_values, full_out, preferred_element_type=jnp.float32)
            return (attended, key_vectors, value_vectors)

        def skipped(caches):
            return (jnp.zeros((tok_rows, model_width), jnp.float32), caches[0], caches[1])

        attended, key_cache, value_cache = lax.cond(
            active, attend, skipped, (key_cache, value_cache)
        )
        outgoing = jnp.einsum(
            "te,td->ed", scatter_table, moe_input, preferred_element_type=jnp.float32
        )
        outgoing = outgoing.astype(jnp.bfloat16).reshape(expert_count, capacity, model_width)
        arrived = lax.all_to_all(outgoing, "expert", split_axis=0, concat_axis=0, tiled=True)
        slot_rows = arrived.reshape(-1, model_width)
        produced = lax.cond(active, feed_rows, blank_rows, slot_rows).reshape(arrived.shape)
        returned = lax.all_to_all(produced, "expert", split_axis=0, concat_axis=0, tiled=True)
        mixed = jnp.dot(
            combine_table, returned.reshape(-1, model_width), preferred_element_type=jnp.float32
        )
        output_rows = (wide_input + attended + mixed).astype(jnp.bfloat16)
        updated = lax.dynamic_update_index_in_dim(stored, output_rows, clipped, 0)
        stored = jnp.where(active, updated, stored)
        inbound = shifted(output_rows, "section", 1)
        return (inbound, key_cache, value_cache, stored)

    initial = (
        jnp.zeros((tok_rows, model_width), jnp.bfloat16),
        jnp.zeros((length, head_size), jnp.bfloat16),
        jnp.zeros((length, head_size), jnp.bfloat16),
        jnp.zeros((micro_count, tok_rows, model_width), jnp.bfloat16),
    )
    finals = lax.fori_loop(0, micro_count + section_count - 1, advance, initial)
    return finals[3][None]


def solution(mesh):
    placed = (
        P(None, "expert", None),
        P("section", None),
        P("section", None),
        P("section", "expert", None),
        P("section", "expert", None),
        P("section", "expert", None),
        P("section", "expert", None),
        P("section", "expert", None, None),
        P("section", "expert", None, None),
        P("section", "expert", None, None),
        P("section", None, "expert", None),
        P("section", None, "expert", None),
    )
    return jax.shard_map(
        shards,
        mesh=mesh,
        in_specs=placed,
        out_specs=P("section", None, "expert", None),
        check_vma=False,
    )
```

profile of v0, /device:TPU:13, one launch (start us, length us, event | category | flops | bytes accessed | tf_op | source)
XLA Modules:
  0.0 1033.6 jit_solution(5070451524895726768)
XLA Ops:
  17.4 41.9 %all_gather.13 = bf16[1,2048,128]{2,1,0:T(8,128)(2,1)S(1)} all-gather(bf16[1,64,128]{2,1,0:T(8,128)(2,1)S(1)} %copy-done.3), channel_id=1, replica_groups=mesh['section'=8,'expert'=32] {'expert'}, dimensions={1}, use_global_device_ids=true | all-gather | bytes 540672 | tf_op jit(solution)/shard_map/all_gather | solution.py:71
  59.2 39.1 %all_gather.12 = bf16[1,2048,128]{2,1,0:T(8,128)(2,1)S(1)} all-gather(bf16[1,64,128]{2,1,0:T(8,128)(2,1)S(1)} %copy-done.4), channel_id=1, replica_groups=mesh['section'=8,'expert'=32] {'expert'}, dimensions={1}, use_global_device_ids=true | all-gather | bytes 540672 | tf_op jit(solution)/shard_map/all_gather | solution.py:72
  98.4 73.4 %all-gather.5.cloned.1.call-done = bf16[1,1024,2048]{2,1,0:T(8,128)(2,1)} async-done(((bf16[1,32,2048]{2,1,0:T(8,128)(2,1)}), bf16[1,1024,2048]{2,1,0:T(8,128)(2,1)}) %all-gather.5.cloned.1.call-update) | async-done | bytes 4194320 | tf_op jit(solution)/shard_map/all_gather | solution.py:73
  171.8 854.1 %while.20 = (s32[]{:T(128)}, bf16[32,2048]{1,0:T(8,128)(2,1)S(1)}, bf16[128,128]{1,0:T(8,128)(2,1)S(1)}, bf16[128,128]{1,0:T(8,128)(2,1)S(1)}, bf16[4,32,2048]{2...) while((s32[]{:T(128)}, bf16[32,2048]{1,0:T(8,128)(2,1)S(1)}, ...), condition=%wide.region_14.15_spmd, body=%wide.region_0.14_spmd.sunk | while | flops 2613929216 | bytes 35623652 | solution.py:183
  183.2 24.0 %all-to-all-done = bf16[32,8,2048]{2,1,0:T(8,128)(2,1)S(1)} async-done(((bf16[32,8,2048]{2,1,0:T(8,128)(2,1)}), bf16[32,8,2048]{2,1,0:T(8,128)(2,1)S(1)}, u32[]{:S(2)}, u32[]{:S(2)}) %all-to-all-start) | async-done | bytes 1048608 | tf_op jit(solution)/shard_map/while/body/eval_jaxpr/all_to_all | solution.py:164
  215.2 24.0 %all-to-all-done.1 = bf16[32,8,2048]{2,1,0:T(8,128)(2,1)S(1)} async-done(((bf16[32,8,2048]{2,1,0:T(8,128)(2,1)}), bf16[32,8,2048]{2,1,0:T(8,128)(2,1)S(1)}, u32[]{:S(2)}, u32[]{:S(2)}) %all-to-all-start.1) | async-done | bytes 1048608 | tf_op jit(solution)/shard_map/while/body/eval_jaxpr/all_to_all | solution.py:167
  258.4 26.1 %all-to-all-done = bf16[32,8,2048]{2,1,0:T(8,128)(2,1)S(1)} async-done(((bf16[32,8,2048]{2,1,0:T(8,128)(2,1)}), bf16[32,8,2048]{2,1,0:T(8,128)(2,1)S(1)}, u32[]{:S(2)}, u32[]{:S(2)}) %all-to-all-start) | async-done | bytes 1048608 | tf_op jit(solution)/shard_map/while/body/eval_jaxpr/all_to_all | solution.py:164
  291.9 26.1 %all-to-all-done.1 = bf16[32,8,2048]{2,1,0:T(8,128)(2,1)S(1)} async-done(((bf16[32,8,2048]{2,1,0:T(8,128)(2,1)}), bf16[32,8,2048]{2,1,0:T(8,128)(2,1)S(1)}, u32[]{:S(2)}, u32[]{:S(2)}) %all-to-all-start.1) | async-done | bytes 1048608 | tf_op jit(solution)/shard_map/while/body/eval_jaxpr/all_to_all | solution.py:167
  333.2 24.1 %all-to-all-done = bf16[32,8,2048]{2,1,0:T(8,128)(2,1)S(1)} async-done(((bf16[32,8,2048]{2,1,0:T(8,128)(2,1)}), bf16[32,8,2048]{2,1,0:T(8,128)(2,1)S(1)}, u32[]{:S(2)}, u32[]{:S(2)}) %all-to-all-start) | async-done | bytes 1048608 | tf_op jit(solution)/shard_map/while/body/eval_jaxpr/all_to_all | solution.py:164
  364.8 23.9 %all-to-all-done.1 = bf16[32,8,2048]{2,1,0:T(8,128)(2,1)S(1)} async-done(((bf16[32,8,2048]{2,1,0:T(8,128)(2,1)}), bf16[32,8,2048]{2,1,0:T(8,128)(2,1)S(1)}, u32[]{:S(2)}, u32[]{:S(2)}) %all-to-all-start.1) | async-done | bytes 1048608 | tf_op jit(solution)/shard_map/while/body/eval_jaxpr/all_to_all | solution.py:167
  406.2 24.1 %all-to-all-done = bf16[32,8,2048]{2,1,0:T(8,128)(2,1)S(1)} async-done(((bf16[32,8,2048]{2,1,0:T(8,128)(2,1)}), bf16[32,8,2048]{2,1,0:T(8,128)(2,1)S(1)}, u32[]{:S(2)}, u32[]{:S(2)}) %all-to-all-start) | async-done | bytes 1048608 | tf_op jit(solution)/shard_map/while/body/eval_jaxpr/all_to_all | solution.py:164
  437.8 23.9 %all-to-all-done.1 = bf16[32,8,2048]{2,1,0:T(8,128)(2,1)S(1)} async-done(((bf16[32,8,2048]{2,1,0:T(8,128)(2,1)}), bf16[32,8,2048]{2,1,0:T(8,128)(2,1)S(1)}, u32[]{:S(2)}, u32[]{:S(2)}) %all-to-all-start.1) | async-done | bytes 1048608 | tf_op jit(solution)/shard_map/while/body/eval_jaxpr/all_to_all | solution.py:167
  479.1 24.1 %all-to-all-done = bf16[32,8,2048]{2,1,0:T(8,128)(2,1)S(1)} async-done(((bf16[32,8,2048]{2,1,0:T(8,128)(2,1)}), bf16[32,8,2048]{2,1,0:T(8,128)(2,1)S(1)}, u32[]{:S(2)}, u32[]{:S(2)}) %all-to-all-start) | async-done | bytes 1048608 | tf_op jit(solution)/shard_map/while/body/eval_jaxpr/all_to_all | solution.py:164
  510.7 17.3 %all-to-all-done.1 = bf16[32,8,2048]{2,1,0:T(8,128)(2,1)S(1)} async-done(((bf16[32,8,2048]{2,1,0:T(8,128)(2,1)}), bf16[32,8,2048]{2,1,0:T(8,128)(2,1)S(1)}, u32[]{:S(2)}, u32[]{:S(2)}) %all-to-all-start.1) | async-done | bytes 1048608 | tf_op jit(solution)/shard_map/while/body/eval_jaxpr/all_to_all | solution.py:167
  528.3 10.6 %collective-permute-start = (bf16[32,2048]{1,0:T(8,128)(2,1)S(1)}, bf16[32,2048]{1,0:T(8,128)(2,1)S(1)}, u32[]{:S(2)}, u32[]{:S(2)}) collective-permute-start(bf16[32,2048]{1,0:T(8,128)(2,1)S(1)} %get-tuple-element.610), channel_id=1, source_target_pairs={{0,32},{32,64},{64,96},{96,128},{128,160},{160,192},{192,224},{1,3... | collective-permute-start | bytes 393224 | tf_op jit(solution)/shard_map/while/body/eval_jaxpr/ppermute | solution.py:12
  555.7 21.7 %all-to-all-done = bf16[32,8,2048]{2,1,0:T(8,128)(2,1)S(1)} async-done(((bf16[32,8,2048]{2,1,0:T(8,128)(2,1)}), bf16[32,8,2048]{2,1,0:T(8,128)(2,1)S(1)}, u32[]{:S(2)}, u32[]{:S(2)}) %all-to-all-start) | async-done | bytes 1048608 | tf_op jit(solution)/shard_map/while/body/eval_jaxpr/all_to_all | solution.py:164
  577.5 11.4 %conditional.4 = (bf16[256,2048]{1,0:T(8,128)(2,1)}) conditional(s32[]{:T(128)} %convert_element_type.170, () %tuple.60, (bf16[32,8,2048]{2,1,0:T(8,128)(2,1)S(1)}, bf16[2048,704]{1,0:T(8,128)(2,1)}, bf16[2048,704]{1,0:T(8,128)(2,1)}, bf16[704,2048]{1,0:T(8,128)(2,1)}) %tuple.61), branch_computations={%region_12.12_spmd, %region_13.13_spmd} | conditional | flops 2216198144 | bytes 13238280 | solution.py:166
  603.3 13.9 %all-to-all-done.1 = bf16[32,8,2048]{2,1,0:T(8,128)(2,1)S(1)} async-done(((bf16[32,8,2048]{2,1,0:T(8,128)(2,1)}), bf16[32,8,2048]{2,1,0:T(8,128)(2,1)S(1)}, u32[]{:S(2)}, u32[]{:S(2)}) %all-to-all-start.1) | async-done | bytes 1048608 | tf_op jit(solution)/shard_map/while/body/eval_jaxpr/all_to_all | solution.py:167
  636.9 18.4 %all-to-all-done = bf16[32,8,2048]{2,1,0:T(8,128)(2,1)S(1)} async-done(((bf16[32,8,2048]{2,1,0:T(8,128)(2,1)}), bf16[32,8,2048]{2,1,0:T(8,128)(2,1)S(1)}, u32[]{:S(2)}, u32[]{:S(2)}) %all-to-all-start) | async-done | bytes 1048608 | tf_op jit(solution)/shard_map/while/body/eval_jaxpr/all_to_all | solution.py:164
  655.3 11.4 %conditional.4 = (bf16[256,2048]{1,0:T(8,128)(2,1)}) conditional(s32[]{:T(128)} %convert_element_type.170, () %tuple.60, (bf16[32,8,2048]{2,1,0:T(8,128)(2,1)S(1)}, bf16[2048,704]{1,0:T(8,128)(2,1)}, bf16[2048,704]{1,0:T(8,128)(2,1)}, bf16[704,2048]{1,0:T(8,128)(2,1)}) %tuple.61), branch_computations={%region_12.12_spmd, %region_13.13_spmd} | conditional | flops 2216198144 | bytes 13238280 | solution.py:166
  692.7 12.3 %collective-permute-done = bf16[32,2048]{1,0:T(8,128)(2,1)S(1)} collective-permute-done((bf16[32,2048]{1,0:T(8,128)(2,1)S(1)}, bf16[32,2048]{1,0:T(8,128)(2,1)S(1)}, u32[]{:S(2)}, u32[]{:S(2)}) %collective-permute-start) | collective-permute-done | bytes 131104 | tf_op jit(solution)/shard_map/while/body/eval_jaxpr/ppermute | solution.py:12
  714.1 17.4 %all-to-all-done = bf16[32,8,2048]{2,1,0:T(8,128)(2,1)S(1)} async-done(((bf16[32,8,2048]{2,1,0:T(8,128)(2,1)}), bf16[32,8,2048]{2,1,0:T(8,128)(2,1)S(1)}, u32[]{:S(2)}, u32[]{:S(2)}) %all-to-all-start) | async-done | bytes 1048608 | tf_op jit(solution)/shard_map/while/body/eval_jaxpr/all_to_all | solution.py:164
  731.4 11.4 %conditional.4 = (bf16[256,2048]{1,0:T(8,128)(2,1)}) conditional(s32[]{:T(128)} %convert_element_type.170, () %tuple.60, (bf16[32,8,2048]{2,1,0:T(8,128)(2,1)S(1)}, bf16[2048,704]{1,0:T(8,128)(2,1)}, bf16[2048,704]{1,0:T(8,128)(2,1)}, bf16[704,2048]{1,0:T(8,128)(2,1)}) %tuple.61), branch_computations={%region_12.12_spmd, %region_13.13_spmd} | conditional | flops 2216198144 | bytes 13238280 | solution.py:166
  755.7 12.1 %all-to-all-done.1 = bf16[32,8,2048]{2,1,0:T(8,128)(2,1)S(1)} async-done(((bf16[32,8,2048]{2,1,0:T(8,128)(2,1)}), bf16[32,8,2048]{2,1,0:T(8,128)(2,1)S(1)}, u32[]{:S(2)}, u32[]{:S(2)}) %all-to-all-start.1) | async-done | bytes 1048608 | tf_op jit(solution)/shard_map/while/body/eval_jaxpr/all_to_all | solution.py:167
  775.0 24.2 %collective-permute-done = bf16[32,2048]{1,0:T(8,128)(2,1)S(1)} collective-permute-done((bf16[32,2048]{1,0:T(8,128)(2,1)S(1)}, bf16[32,2048]{1,0:T(8,128)(2,1)S(1)}, u32[]{:S(2)}, u32[]{:S(2)}) %collective-permute-start) | collective-permute-done | bytes 131104 | tf_op jit(solution)/shard_map/while/body/eval_jaxpr/ppermute | solution.py:12
  808.3 24.1 %all-to-all-done = bf16[32,8,2048]{2,1,0:T(8,128)(2,1)S(1)} async-done(((bf16[32,8,2048]{2,1,0:T(8,128)(2,1)}), bf16[32,8,2048]{2,1,0:T(8,128)(2,1)S(1)}, u32[]{:S(2)}, u32[]{:S(2)}) %all-to-all-start) | async-done | bytes 1048608 | tf_op jit(solution)/shard_map/while/body/eval_jaxpr/all_to_all | solution.py:164
  832.4 11.4 %conditional.4 = (bf16[256,2048]{1,0:T(8,128)(2,1)}) conditional(s32[]{:T(128)} %convert_element_type.170, () %tuple.60, (bf16[32,8,2048]{2,1,0:T(8,128)(2,1)S(1)}, bf16[2048,704]{1,0:T(8,128)(2,1)}, bf16[2048,704]{1,0:T(8,128)(2,1)}, bf16[704,2048]{1,0:T(8,128)(2,1)}) %tuple.61), branch_computations={%region_12.12_spmd, %region_13.13_spmd} | conditional | flops 2216198144 | bytes 13238280 | solution.py:166
  858.0 15.1 %all-to-all-done.1 = bf16[32,8,2048]{2,1,0:T(8,128)(2,1)S(1)} async-done(((bf16[32,8,2048]{2,1,0:T(8,128)(2,1)}), bf16[32,8,2048]{2,1,0:T(8,128)(2,1)S(1)}, u32[]{:S(2)}, u32[]{:S(2)}) %all-to-all-start.1) | async-done | bytes 1048608 | tf_op jit(solution)/shard_map/while/body/eval_jaxpr/all_to_all | solution.py:167
  886.3 28.2 %all-to-all-done = bf16[32,8,2048]{2,1,0:T(8,128)(2,1)S(1)} async-done(((bf16[32,8,2048]{2,1,0:T(8,128)(2,1)}), bf16[32,8,2048]{2,1,0:T(8,128)(2,1)S(1)}, u32[]{:S(2)}, u32[]{:S(2)}) %all-to-all-start) | async-done | bytes 1048608 | tf_op jit(solution)/shard_map/while/body/eval_jaxpr/all_to_all | solution.py:164
  920.7 26.4 %all-to-all-done.1 = bf16[32,8,2048]{2,1,0:T(8,128)(2,1)S(1)} async-done(((bf16[32,8,2048]{2,1,0:T(8,128)(2,1)}), bf16[32,8,2048]{2,1,0:T(8,128)(2,1)S(1)}, u32[]{:S(2)}, u32[]{:S(2)}) %all-to-all-start.1) | async-done | bytes 1048608 | tf_op jit(solution)/shard_map/while/body/eval_jaxpr/all_to_all | solution.py:167
  962.1 24.1 %all-to-all-done = bf16[32,8,2048]{2,1,0:T(8,128)(2,1)S(1)} async-done(((bf16[32,8,2048]{2,1,0:T(8,128)(2,1)}), bf16[32,8,2048]{2,1,0:T(8,128)(2,1)S(1)}, u32[]{:S(2)}, u32[]{:S(2)}) %all-to-all-start) | async-done | bytes 1048608 | tf_op jit(solution)/shard_map/while/body/eval_jaxpr/all_to_all | solution.py:164
  993.7 23.9 %all-to-all-done.1 = bf16[32,8,2048]{2,1,0:T(8,128)(2,1)S(1)} async-done(((bf16[32,8,2048]{2,1,0:T(8,128)(2,1)}), bf16[32,8,2048]{2,1,0:T(8,128)(2,1)S(1)}, u32[]{:S(2)}, u32[]{:S(2)}) %all-to-all-start.1) | async-done | bytes 1048608 | tf_op jit(solution)/shard_map/while/body/eval_jaxpr/all_to_all | solution.py:167
  (387 shorter events, 393.9 us)
Async XLA Ops:
  6.5 91.8 %all-gather.3.cloned.1.call-start = ((), (), s32[]{:S(2)}) async-start(), calls=%async_computation.2 | async-start | bytes 4325376 | tf_op jit(solution)/shard_map/all_gather | solution.py:70
  7.3 164.5 %all-gather.5.cloned.1.call-start = ((), (), s32[]{:S(2)}) async-start(), calls=%async_computation.3 | async-start | bytes 4325376 | tf_op jit(solution)/shard_map/all_gather | solution.py:73
  175.9 31.3 %all-to-all-start = ((bf16[32,8,2048]{2,1,0:T(8,128)(2,1)}), bf16[32,8,2048]{2,1,0:T(8,128)(2,1)S(1)}, u32[]{:S(2)}, u32[]{:S(2)}) async-start(bf16[32,8,2048]{2,1,0:T(8,128)(2,1)} %fusion.71), calls=%async_computation | async-start | bytes 2097152 | tf_op jit(solution)/shard_map/while/body/eval_jaxpr/all_to_all | solution.py:164
  208.4 30.8 %all-to-all-start.1 = ((bf16[32,8,2048]{2,1,0:T(8,128)(2,1)}), bf16[32,8,2048]{2,1,0:T(8,128)(2,1)S(1)}, u32[]{:S(2)}, u32[]{:S(2)}) async-start(bf16[32,8,2048]{2,1,0:T(8,128)(2,1)} %bitcast.125), calls=%async_computation.1 | async-start | bytes 2097152 | tf_op jit(solution)/shard_map/while/body/eval_jaxpr/all_to_all | solution.py:167
  239.5 9.9 collective-permute-start
  253.4 31.2 %all-to-all-start = ((bf16[32,8,2048]{2,1,0:T(8,128)(2,1)}), bf16[32,8,2048]{2,1,0:T(8,128)(2,1)S(1)}, u32[]{:S(2)}, u32[]{:S(2)}) async-start(bf16[32,8,2048]{2,1,0:T(8,128)(2,1)} %fusion.71), calls=%async_computation | async-start | bytes 2097152 | tf_op jit(solution)/shard_map/while/body/eval_jaxpr/all_to_all | solution.py:164
  285.7 32.3 %all-to-all-start.1 = ((bf16[32,8,2048]{2,1,0:T(8,128)(2,1)}), bf16[32,8,2048]{2,1,0:T(8,128)(2,1)S(1)}, u32[]{:S(2)}, u32[]{:S(2)}) async-start(bf16[32,8,2048]{2,1,0:T(8,128)(2,1)} %bitcast.125), calls=%async_computation.1 | async-start | bytes 2097152 | tf_op jit(solution)/shard_map/while/body/eval_jaxpr/all_to_all | solution.py:167
  328.2 29.1 %all-to-all-start = ((bf16[32,8,2048]{2,1,0:T(8,128)(2,1)}), bf16[32,8,2048]{2,1,0:T(8,128)(2,1)S(1)}, u32[]{:S(2)}, u32[]{:S(2)}) async-start(bf16[32,8,2048]{2,1,0:T(8,128)(2,1)} %fusion.71), calls=%async_computation | async-start | bytes 2097152 | tf_op jit(solution)/shard_map/while/body/eval_jaxpr/all_to_all | solution.py:164
  358.4 30.3 %all-to-all-start.1 = ((bf16[32,8,2048]{2,1,0:T(8,128)(2,1)}), bf16[32,8,2048]{2,1,0:T(8,128)(2,1)S(1)}, u32[]{:S(2)}, u32[]{:S(2)}) async-start(bf16[32,8,2048]{2,1,0:T(8,128)(2,1)} %bitcast.125), calls=%async_computation.1 | async-start | bytes 2097152 | tf_op jit(solution)/shard_map/while/body/eval_jaxpr/all_to_all | solution.py:167
  389.0 8.1 collective-permute-start
  401.2 29.1 %all-to-all-start = ((bf16[32,8,2048]{2,1,0:T(8,128)(2,1)}), bf16[32,8,2048]{2,1,0:T(8,128)(2,1)S(1)}, u32[]{:S(2)}, u32[]{:S(2)}) async-start(bf16[32,8,2048]{2,1,0:T(8,128)(2,1)} %fusion.71), calls=%async_computation | async-start | bytes 2097152 | tf_op jit(solution)/shard_map/while/body/eval_jaxpr/all_to_all | solution.py:164
  431.3 30.3 %all-to-all-start.1 = ((bf16[32,8,2048]{2,1,0:T(8,128)(2,1)}), bf16[32,8,2048]{2,1,0:T(8,128)(2,1)S(1)}, u32[]{:S(2)}, u32[]{:S(2)}) async-start(bf16[32,8,2048]{2,1,0:T(8,128)(2,1)} %bitcast.125), calls=%async_computation.1 | async-start | bytes 2097152 | tf_op jit(solution)/shard_map/while/body/eval_jaxpr/all_to_all | solution.py:167
  462.0 8.1 collective-permute-start
  474.1 29.1 %all-to-all-start = ((bf16[32,8,2048]{2,1,0:T(8,128)(2,1)}), bf16[32,8,2048]{2,1,0:T(8,128)(2,1)S(1)}, u32[]{:S(2)}, u32[]{:S(2)}) async-start(bf16[32,8,2048]{2,1,0:T(8,128)(2,1)} %fusion.71), calls=%async_computation | async-start | bytes 2097152 | tf_op jit(solution)/shard_map/while/body/eval_jaxpr/all_to_all | solution.py:164
  504.3 23.7 %all-to-all-start.1 = ((bf16[32,8,2048]{2,1,0:T(8,128)(2,1)}), bf16[32,8,2048]{2,1,0:T(8,128)(2,1)S(1)}, u32[]{:S(2)}, u32[]{:S(2)}) async-start(bf16[32,8,2048]{2,1,0:T(8,128)(2,1)} %bitcast.125), calls=%async_computation.1 | async-start | bytes 2097152 | tf_op jit(solution)/shard_map/while/body/eval_jaxpr/all_to_all | solution.py:167
  528.3 18.3 %collective-permute-start = (bf16[32,2048]{1,0:T(8,128)(2,1)S(1)}, bf16[32,2048]{1,0:T(8,128)(2,1)S(1)}, u32[]{:S(2)}, u32[]{:S(2)}) collective-permute-start(bf16[32,2048]{1,0:T(8,128)(2,1)S(1)} %get-tuple-element.610), channel_id=1, source_target_pairs={{0,32},{32,64},{64,96},{96,128},{128,160},{160,192},{192,224},{1,3... | collective-permute-start | bytes 393224 | tf_op jit(solution)/shard_map/while/body/eval_jaxpr/ppermute | solution.py:12
  550.7 26.8 %all-to-all-start = ((bf16[32,8,2048]{2,1,0:T(8,128)(2,1)}), bf16[32,8,2048]{2,1,0:T(8,128)(2,1)S(1)}, u32[]{:S(2)}, u32[]{:S(2)}) async-start(bf16[32,8,2048]{2,1,0:T(8,128)(2,1)} %fusion.71), calls=%async_computation | async-start | bytes 2097152 | tf_op jit(solution)/shard_map/while/body/eval_jaxpr/all_to_all | solution.py:164
  588.9 28.4 %all-to-all-start.1 = ((bf16[32,8,2048]{2,1,0:T(8,128)(2,1)}), bf16[32,8,2048]{2,1,0:T(8,128)(2,1)S(1)}, u32[]{:S(2)}, u32[]{:S(2)}) async-start(bf16[32,8,2048]{2,1,0:T(8,128)(2,1)} %bitcast.125), calls=%async_computation.1 | async-start | bytes 2097152 | tf_op jit(solution)/shard_map/while/body/eval_jaxpr/all_to_all | solution.py:167
  617.5 10.3 collective-permute-start
  631.8 23.4 %all-to-all-start = ((bf16[32,8,2048]{2,1,0:T(8,128)(2,1)}), bf16[32,8,2048]{2,1,0:T(8,128)(2,1)S(1)}, u32[]{:S(2)}, u32[]{:S(2)}) async-start(bf16[32,8,2048]{2,1,0:T(8,128)(2,1)} %fusion.71), calls=%async_computation | async-start | bytes 2097152 | tf_op jit(solution)/shard_map/while/body/eval_jaxpr/all_to_all | solution.py:164
  666.6 23.8 %all-to-all-start.1 = ((bf16[32,8,2048]{2,1,0:T(8,128)(2,1)}), bf16[32,8,2048]{2,1,0:T(8,128)(2,1)S(1)}, u32[]{:S(2)}, u32[]{:S(2)}) async-start(bf16[32,8,2048]{2,1,0:T(8,128)(2,1)} %bitcast.125), calls=%async_computation.1 | async-start | bytes 2097152 | tf_op jit(solution)/shard_map/while/body/eval_jaxpr/all_to_all | solution.py:167
  690.7 14.2 %collective-permute-start = (bf16[32,2048]{1,0:T(8,128)(2,1)S(1)}, bf16[32,2048]{1,0:T(8,128)(2,1)S(1)}, u32[]{:S(2)}, u32[]{:S(2)}) collective-permute-start(bf16[32,2048]{1,0:T(8,128)(2,1)S(1)} %get-tuple-element.610), channel_id=1, source_target_pairs={{0,32},{32,64},{64,96},{96,128},{128,160},{160,192},{192,224},{1,3... | collective-permute-start | bytes 393224 | tf_op jit(solution)/shard_map/while/body/eval_jaxpr/ppermute | solution.py:12
  709.1 22.4 %all-to-all-start = ((bf16[32,8,2048]{2,1,0:T(8,128)(2,1)}), bf16[32,8,2048]{2,1,0:T(8,128)(2,1)S(1)}, u32[]{:S(2)}, u32[]{:S(2)}) async-start(bf16[32,8,2048]{2,1,0:T(8,128)(2,1)} %fusion.71), calls=%async_computation | async-start | bytes 2097152 | tf_op jit(solution)/shard_map/while/body/eval_jaxpr/all_to_all | solution.py:164
  742.8 25.1 %all-to-all-start.1 = ((bf16[32,8,2048]{2,1,0:T(8,128)(2,1)}), bf16[32,8,2048]{2,1,0:T(8,128)(2,1)S(1)}, u32[]{:S(2)}, u32[]{:S(2)}) async-start(bf16[32,8,2048]{2,1,0:T(8,128)(2,1)} %bitcast.125), calls=%async_computation.1 | async-start | bytes 2097152 | tf_op jit(solution)/shard_map/while/body/eval_jaxpr/all_to_all | solution.py:167
  768.2 31.0 %collective-permute-start = (bf16[32,2048]{1,0:T(8,128)(2,1)S(1)}, bf16[32,2048]{1,0:T(8,128)(2,1)S(1)}, u32[]{:S(2)}, u32[]{:S(2)}) collective-permute-start(bf16[32,2048]{1,0:T(8,128)(2,1)S(1)} %get-tuple-element.610), channel_id=1, source_target_pairs={{0,32},{32,64},{64,96},{96,128},{128,160},{160,192},{192,224},{1,3... | collective-permute-start | bytes 393224 | tf_op jit(solution)/shard_map/while/body/eval_jaxpr/ppermute | solution.py:12
  803.3 29.1 %all-to-all-start = ((bf16[32,8,2048]{2,1,0:T(8,128)(2,1)}), bf16[32,8,2048]{2,1,0:T(8,128)(2,1)S(1)}, u32[]{:S(2)}, u32[]{:S(2)}) async-start(bf16[32,8,2048]{2,1,0:T(8,128)(2,1)} %fusion.71), calls=%async_computation | async-start | bytes 2097152 | tf_op jit(solution)/shard_map/while/body/eval_jaxpr/all_to_all | solution.py:164
  843.7 29.3 %all-to-all-start.1 = ((bf16[32,8,2048]{2,1,0:T(8,128)(2,1)}), bf16[32,8,2048]{2,1,0:T(8,128)(2,1)S(1)}, u32[]{:S(2)}, u32[]{:S(2)}) async-start(bf16[32,8,2048]{2,1,0:T(8,128)(2,1)} %bitcast.125), calls=%async_computation.1 | async-start | bytes 2097152 | tf_op jit(solution)/shard_map/while/body/eval_jaxpr/all_to_all | solution.py:167
  881.3 33.2 %all-to-all-start = ((bf16[32,8,2048]{2,1,0:T(8,128)(2,1)}), bf16[32,8,2048]{2,1,0:T(8,128)(2,1)S(1)}, u32[]{:S(2)}, u32[]{:S(2)}) async-start(bf16[32,8,2048]{2,1,0:T(8,128)(2,1)} %fusion.71), calls=%async_computation | async-start | bytes 2097152 | tf_op jit(solution)/shard_map/while/body/eval_jaxpr/all_to_all | solution.py:164
  915.6 31.6 %all-to-all-start.1 = ((bf16[32,8,2048]{2,1,0:T(8,128)(2,1)}), bf16[32,8,2048]{2,1,0:T(8,128)(2,1)S(1)}, u32[]{:S(2)}, u32[]{:S(2)}) async-start(bf16[32,8,2048]{2,1,0:T(8,128)(2,1)} %bitcast.125), calls=%async_computation.1 | async-start | bytes 2097152 | tf_op jit(solution)/shard_map/while/body/eval_jaxpr/all_to_all | solution.py:167
  957.1 29.1 %all-to-all-start = ((bf16[32,8,2048]{2,1,0:T(8,128)(2,1)}), bf16[32,8,2048]{2,1,0:T(8,128)(2,1)S(1)}, u32[]{:S(2)}, u32[]{:S(2)}) async-start(bf16[32,8,2048]{2,1,0:T(8,128)(2,1)} %fusion.71), calls=%async_computation | async-start | bytes 2097152 | tf_op jit(solution)/shard_map/while/body/eval_jaxpr/all_to_all | solution.py:164
  987.2 30.3 %all-to-all-start.1 = ((bf16[32,8,2048]{2,1,0:T(8,128)(2,1)}), bf16[32,8,2048]{2,1,0:T(8,128)(2,1)S(1)}, u32[]{:S(2)}, u32[]{:S(2)}) async-start(bf16[32,8,2048]{2,1,0:T(8,128)(2,1)} %bitcast.125), calls=%async_computation.1 | async-start | bytes 2097152 | tf_op jit(solution)/shard_map/while/body/eval_jaxpr/all_to_all | solution.py:167
  1017.9 8.1 collective-permute-start
  (10 other events, 556.9 us)
Sparse Core Ops, SparseCore 0:
  9.9 80.3 all-gather.2
  92.9 78.7 all-gather.4
where the time goes:
time: 1040 us; the launch traced here: 1030 us
  waiting for transfers between devices  624 us (60%)
  starting transfers between devices  172 us (17%)
  matrix products  94.8 us (9%)
  blocking collectives  80.9 us (8%)
  local copies, waits for them, and re-layouts  24.2 us (2%)
  other arithmetic  23.1 us (2%)
  between operations  13.5 us (1%)
    all_to_all x11, waiting for transfers between devices, advance(): lax.all_to_all(outgoing, 'expert', split_axis=0, concat_axis=0, tiled=True)  256 us
    all_to_all x11, waiting for transfers between devices, advance(): lax.all_to_all(produced, 'expert', split_axis=0, concat_axis=0, tiled=True)  217 us
    ppermute x11, waiting for transfers between devices, shifted(): lax.ppermute(value, axis, [(source, source + steps) for source in range(i...  76.1 us
    all_gather x1, waiting for transfers between devices, shards(): lax.all_gather(out_weight, 'expert', axis=1, tiled=True)  73.4 us
    all_to_all x11, starting transfers between devices, advance(): lax.all_to_all(produced, 'expert', split_axis=0, concat_axis=0, tiled=True)  67.3 us
    all_to_all x11, starting transfers between devices, advance(): lax.all_to_all(outgoing, 'expert', split_axis=0, concat_axis=0, tiled=True)  57.4 us
    ppermute x11, starting transfers between devices, shifted(): lax.ppermute(value, axis, [(source, source + steps) for source in range(i...  47.1 us
    all_gather x1, blocking collectives, shards(): lax.all_gather(key_weight, 'expert', axis=1, tiled=True)  41.9 us
  transfers between devices with their start and end apart: 35, of which 34 were waited for; matrix products, arithmetic and copies ran while one was open for 4% of the time, Pallas kernels for 0%

commit v1 on v0

v1 whole, which is shorter than its diff:
```python
import jax
import jax.numpy as jnp
from jax import lax
from jax.experimental import pallas as pl
from jax.experimental.pallas import tpu as pltpu
from jax.sharding import PartitionSpec as P

epsilon = 1e-06

POSITION = (0, 6, 2, 4, 7, 3, 1, 5)
LAYER_AT = tuple(POSITION.index(place) for place in range(8))
MOVES = [(layer, place) for layer, place in enumerate(POSITION) if layer != place]
HOME = [(place, layer) for layer, place in MOVES]
RELAY = [(POSITION[layer], POSITION[layer + 1]) for layer in range(7)]

CHUNKS = 4


def rms_normed(wide, gain_vector):
    scale = lax.rsqrt(jnp.mean(wide * wide, axis=-1, keepdims=True) + epsilon)
    return (wide * scale * gain_vector).astype(jnp.bfloat16)


def expert_kernel(
    moved_ref,
    rows_ref,
    gate_own,
    up_own,
    down_own,
    gate_new,
    up_new,
    down_new,
    out_ref,
    gate_buf,
    up_buf,
    down_buf,
    gate_acc,
    up_acc,
    gate_sem,
    up_sem,
    down_sem,
):
    depth = gate_buf.shape[1]
    width = down_buf.shape[2]

    def copies(gate_hbm, up_hbm, down_hbm):
        firsts, lasts = [], []
        for step in range(CHUNKS):
            part = pl.ds(step * depth, depth)
            firsts.append(
                (
                    pltpu.make_async_copy(
                        gate_hbm.at[part, :], gate_buf.at[step], gate_sem.at[step]
                    ),
                    pltpu.make_async_copy(up_hbm.at[part, :], up_buf.at[step], up_sem.at[step]),
                )
            )
        for step in range(CHUNKS):
            part = pl.ds(step * width, width)
            lasts.append(
                pltpu.make_async_copy(down_hbm.at[:, part], down_buf.at[step], down_sem.at[step])
            )
        return firsts, lasts

    def start(firsts, lasts):
        for first, second in firsts:
            first.start()
            second.start()
        for copy in lasts:
            copy.start()

    moved = moved_ref[0]

    @pl.when(moved == 0)
    def _():
        start(*copies(gate_own, up_own, down_own))

    @pl.when(moved != 0)
    def _():
        start(*copies(gate_new, up_new, down_new))

    firsts, lasts = copies(gate_own, up_own, down_own)
    for step in range(CHUNKS):
        first, second = firsts[step]
        rows = rows_ref[:, step * depth : (step + 1) * depth]
        first.wait()
        gated = jnp.dot(rows, gate_buf[step], preferred_element_type=jnp.float32)
        second.wait()
        lifted = jnp.dot(rows, up_buf[step], preferred_element_type=jnp.float32)
        if step == 0:
            gate_acc[...] = gated
            up_acc[...] = lifted
        else:
            gate_acc[...] += gated
            up_acc[...] += lifted
    gated = gate_acc[...]
    hidden = (gated * jax.nn.sigmoid(gated) * up_acc[...]).astype(jnp.bfloat16)
    for step in range(CHUNKS):
        lasts[step].wait()
        out_ref[:, step * width : (step + 1) * width] = jnp.dot(
            hidden, down_buf[step], preferred_element_type=jnp.float32
        ).astype(jnp.bfloat16)


def expert_rows(moved, rows, own, new):
    count, model_width = rows.shape
    hidden_width = own[0].shape[1]
    depth = model_width // CHUNKS
    vmem = pl.BlockSpec(memory_space=pltpu.VMEM)
    anywhere = pl.BlockSpec(memory_space=pl.ANY)
    return pl.pallas_call(
        expert_kernel,
        out_shape=jax.ShapeDtypeStruct((count, model_width), jnp.bfloat16),
        in_specs=[pl.BlockSpec(memory_space=pltpu.SMEM), vmem] + [anywhere] * 6,
        out_specs=vmem,
        scratch_shapes=[
            pltpu.VMEM((CHUNKS, depth, hidden_width), jnp.bfloat16),
            pltpu.VMEM((CHUNKS, depth, hidden_width), jnp.bfloat16),
            pltpu.VMEM((CHUNKS, hidden_width, depth), jnp.bfloat16),
            pltpu.VMEM((count, hidden_width), jnp.float32),
            pltpu.VMEM((count, hidden_width), jnp.float32),
            pltpu.SemaphoreType.DMA((CHUNKS,)),
            pltpu.SemaphoreType.DMA((CHUNKS,)),
            pltpu.SemaphoreType.DMA((CHUNKS,)),
        ],
        compiler_params=pltpu.CompilerParams(vmem_limit_bytes=40 * 2**20),
        cost_estimate=pl.CostEstimate(
            flops=6 * count * model_width * hidden_width,
            bytes_accessed=6 * model_width * hidden_width + 4 * count * model_width,
            transcendentals=count * hidden_width,
        ),
        name="experts",
    )(moved, rows, *own, *new)


def route_tables(picks, codes, expert_count, capacity):
    micro_count, tok_rows, pick_count = picks.shape
    flat_ids = picks.reshape(micro_count, tok_rows * pick_count)
    experts = jnp.arange(expert_count, dtype=jnp.int32)
    matches = (flat_ids[:, :, None] == experts[None, None, :]).astype(jnp.float32)
    order = jnp.arange(tok_rows * pick_count, dtype=jnp.int32)
    earlier = (order[:, None] > order[None, :]).astype(jnp.float32)
    before = jnp.einsum("ij,mje->mie", earlier, matches)
    slot_ranks = jnp.sum(before * matches, axis=2).astype(jnp.int32)
    columns = (flat_ids * capacity + slot_ranks).reshape(micro_count, tok_rows, pick_count)
    slots = jnp.arange(expert_count * capacity, dtype=jnp.int32)
    pick_weights = codes.astype(jnp.float32) / 64.0
    scatter_table = jnp.zeros((micro_count, tok_rows, expert_count * capacity), jnp.float32)
    combine_table = scatter_table
    for pick in range(pick_count):
        onehot = (columns[:, :, pick, None] == slots[None, None, :]).astype(jnp.float32)
        scatter_table = scatter_table + onehot
        combine_table = combine_table + onehot * pick_weights[:, :, pick, None]
    return (scatter_table.astype(jnp.bfloat16), combine_table.astype(jnp.bfloat16))


def shards(
    tokens,
    attn_norm,
    moe_norm,
    query_weight,
    key_weight,
    value_weight,
    out_weight,
    gate_proj,
    up_proj,
    down_proj,
    routes,
    weights_code,
):
    section_count = lax.axis_size("section")
    place = lax.axis_index("section")
    expert_devices = lax.axis_size("expert")
    micro_count, tok_rows, model_width = tokens.shape
    pick_count = routes.shape[3]
    expert_count = expert_devices * gate_proj.shape[1]
    capacity = min(tok_rows, tok_rows * pick_count * 4 // (3 * expert_count))
    layer = jnp.asarray(LAYER_AT, jnp.int32)[place]
    here = layer == place
    moved = (layer != place).astype(jnp.int32).reshape(1)

    def relocated(value):
        return jnp.where(here, value, lax.ppermute(value, "section", MOVES))

    head_size = key_weight.shape[-1]
    head_count = query_weight.shape[-1] // head_size
    half = model_width // 2
    out_shard = out_weight[0]
    packed = jnp.concatenate(
        [
            query_weight[0],
            key_weight[0],
            value_weight[0],
            jnp.concatenate([out_shard[:, :half], out_shard[:, half:]], axis=0),
        ],
        axis=1,
    )
    full = lax.all_gather(relocated(packed), "expert", axis=0, tiled=True)
    tables = relocated(jnp.concatenate([routes[0], weights_code[0]], axis=-1))
    gains = relocated(jnp.concatenate([attn_norm, moe_norm], axis=0))
    attn_gain, moe_gain = gains[0], gains[1]
    scatter_tables, combine_tables = route_tables(
        tables[:, :, :pick_count], tables[:, :, pick_count:], expert_count, capacity
    )
    own = (gate_proj[0, 0], up_proj[0, 0], down_proj[0, 0])
    new = tuple(lax.ppermute(value, "section", MOVES) for value in own)

    score_width = (head_count + 2) * head_size
    length = micro_count * tok_rows
    score_scale = head_size ** (-0.5)

    def attention_weights(full):
        rows = out_shard.shape[0]
        halves = full[:, score_width:].reshape(expert_devices, 2, rows, half)
        halves = halves.transpose(0, 2, 1, 3).reshape(expert_devices * rows, model_width)
        return (full[:, :score_width], halves)

    def mixture(layer_input, block, own, new, moved):
        wide = layer_input.astype(jnp.float32)
        normed = rms_normed(wide, moe_gain)
        scatter_table = lax.dynamic_index_in_dim(scatter_tables, block, 0, keepdims=False)
        combine_table = lax.dynamic_index_in_dim(combine_tables, block, 0, keepdims=False)
        outgoing = jnp.einsum("te,td->ed", scatter_table, normed, preferred_element_type=jnp.float32)
        outgoing = outgoing.astype(jnp.bfloat16).reshape(expert_count, capacity, model_width)
        arrived = lax.all_to_all(outgoing, "expert", split_axis=0, concat_axis=0, tiled=True)
        produced = expert_rows(moved, arrived.reshape(-1, model_width), own, new)
        produced = produced.reshape(arrived.shape)
        returned = lax.all_to_all(produced, "expert", split_axis=0, concat_axis=0, tiled=True)
        return jnp.dot(
            combine_table, returned.reshape(-1, model_width), preferred_element_type=jnp.float32
        )

    def attend(layer_input, block, old_keys, old_values, inner, outer):
        normed = rms_normed(layer_input.astype(jnp.float32), attn_gain)
        projected = jnp.dot(normed, inner, preferred_element_type=jnp.float32)
        projected = projected.astype(jnp.bfloat16)
        query_rows = projected[:, : head_count * head_size]
        query_rows = query_rows.reshape(tok_rows, head_count, head_size)
        new_keys = projected[:, head_count * head_size : (head_count + 1) * head_size]
        new_values = projected[:, (head_count + 1) * head_size :]
        offset = block * tok_rows
        key_vectors = lax.dynamic_update_slice_in_dim(old_keys, new_keys, offset, 0)
        value_vectors = lax.dynamic_update_slice_in_dim(old_values, new_values, offset, 0)
        scores = jnp.einsum(
            "qhd,kd->hqk", query_rows, key_vectors, preferred_element_type=jnp.float32
        )
        scores = scores * score_scale
        positions = offset + jnp.arange(tok_rows, dtype=jnp.int32)
        causal = jnp.arange(length, dtype=jnp.int32)[None, :] <= positions[:, None]
        scores = jnp.where(causal[None], scores, -1e30)
        highest = jnp.max(scores, axis=-1, keepdims=True)
        exponent = jnp.exp(scores - highest)
        probabilities = exponent / jnp.sum(exponent, axis=-1, keepdims=True)
        context = jnp.einsum(
            "hqk,kd->qhd",
            probabilities.astype(jnp.bfloat16),
            value_vectors,
            preferred_element_type=jnp.float32,
        )
        context = context.astype(jnp.bfloat16).reshape(tok_rows, head_count * head_size)
        attended = jnp.dot(context, outer, preferred_element_type=jnp.float32)
        return (attended, key_vectors, value_vectors)

    keys = jnp.zeros((length, head_size), jnp.bfloat16)
    values = jnp.zeros((length, head_size), jnp.bfloat16)
    leading = layer == 0
    first_block = jnp.int32(0)
    first_rows = tokens[0]
    mixed = lax.cond(
        leading,
        lambda rows: mixture(rows, first_block, own, own, jnp.zeros((1,), jnp.int32)),
        lambda rows: jnp.zeros((tok_rows, model_width), jnp.float32),
        first_rows,
    )
    inner, outer = attention_weights(full)

    def first_attend(arrays):
        rows, mixed, keys, values = arrays
        attended, keys, values = attend(rows, first_block, keys, values, inner, outer)
        output_rows = (rows.astype(jnp.float32) + attended + mixed).astype(jnp.bfloat16)
        return (output_rows, keys, values)

    output_rows, keys, values = lax.cond(
        leading,
        first_attend,
        lambda arrays: (arrays[0], arrays[2], arrays[3]),
        (first_rows, mixed, keys, values),
    )
    tick_count = micro_count + section_count - 1
    stored = jnp.zeros((tick_count, tok_rows, model_width), jnp.bfloat16)
    stored = lax.dynamic_update_index_in_dim(stored, output_rows, 0, 0)
    inbound = lax.ppermute(output_rows, "section", RELAY)

    def advance(tick_index, state_carry):
        inbound, keys, values, stored = state_carry
        block_index = tick_index - layer
        active = (block_index >= 0) & (block_index < micro_count)
        block = jnp.clip(block_index, 0, micro_count - 1)

        def work(arrays):
            inbound, keys, values = arrays
            held = lax.dynamic_index_in_dim(tokens, block, 0, keepdims=False)
            layer_input = jnp.where(layer == 0, held, inbound)
            mixed = mixture(layer_input, block, own, new, moved)
            attended, keys, values = attend(layer_input, block, keys, values, inner, outer)
            output_rows = layer_input.astype(jnp.float32) + attended + mixed
            return (output_rows.astype(jnp.bfloat16), keys, values)

        output_rows, keys, values = lax.cond(
            active, work, lambda arrays: arrays, (inbound, keys, values)
        )
        stored = lax.dynamic_update_index_in_dim(stored, output_rows, tick_index, 0)
        inbound = lax.ppermute(output_rows, "section", RELAY)
        return (inbound, keys, values, stored)

    finals = lax.fori_loop(1, tick_count, advance, (inbound, keys, values, stored))
    results = lax.dynamic_slice_in_dim(finals[3], layer, micro_count, 0)
    returned_home = lax.ppermute(results, "section", HOME)
    return jnp.where(here, results, returned_home)[None]


def solution(mesh):
    placed = (
        P(None, "expert", None),
        P("section", None),
        P("section", None),
        P("section", "expert", None),
        P("section", "expert", None),
        P("section", "expert", None),
        P("section", "expert", None),
        P("section", "expert", None, None),
        P("section", "expert", None, None),
        P("section", "expert", None, None),
        P("section", None, "expert", None),
        P("section", None, "expert", None),
    )
    return jax.shard_map(
        shards,
        mesh=mesh,
        in_specs=placed,
        out_specs=P("section", None, "expert", None),
        check_vma=False,
    )
```

time: 1040 us -> 914 us (0.88)
  starting transfers between devices: 172 us -> 51.5 us
  waiting for transfers between devices: 624 us -> 558 us
  local copies, waits for them, and re-layouts: 24.2 us -> 70.8 us
  matrix products: 94.8 us -> 50.4 us
  Pallas kernels: 0 us -> 29.9 us
    ppermute x11 -> x18, waiting for transfers between devices: 76.1 us -> 525 us  [the longest x10 433 us: advance(): inbound = lax.ppermute(output_rows, 'section', RELAY)]
    all_to_all x22 -> x4, waiting for transfers between devices: 473 us -> 27.3 us  [mixture(): lax.all_to_all(produced, 'expert', split_axis=0, concat_axis=0, tiled=True)]
    all_to_all x22 -> x4, starting transfers between devices: 125 us -> 20.3 us  [mixture(): lax.all_to_all(produced, 'expert', split_axis=0, concat_axis=0, tiled=True)]
    all_to_all x0 -> x4, blocking collectives: none -> 90.6 us  [mixture(): lax.all_to_all(outgoing, 'expert', split_axis=0, concat_axis=0, tiled=True)]
    all_gather x2 -> x0, blocking collectives: 80.9 us -> none  [the longest x1 41.9 us: shards(): lax.all_gather(key_weight, 'expert', axis=1, tiled=True)]
    all_gather x2 -> x1, waiting for transfers between devices: 73.4 us -> 5.23 us  [shards(): full = lax.all_gather(relocated(packed), 'expert', axis=0, tiled=True)]
    dot_general x50 -> x21, matrix products: 92.7 us -> 42.3 us  [the longest x4 14.1 us: attend(): projected = jnp.dot(normed, inner, preferred_element_type=jnp.float32)]
    pallas_call x0 -> x4, Pallas kernels: none -> 29.9 us  [expert_rows(): pl.pallas_call(expert_kernel, out_shape=jax.ShapeDtypeStruct((count, mode...]
  transfers between devices with their start and end apart: 35 -> 23, of which waited for: 34 -> 18; matrix products, arithmetic and copies ran while one was open for 4% -> 10% of each run, Pallas kernels for 0% -> 0%
where the time goes in v1:
time: 914 us; the launch traced here: 908 us
  waiting for transfers between devices  558 us (61%)
  blocking collectives  90.6 us (10%)
  local copies, waits for them, and re-layouts  70.8 us (8%)
  starting transfers between devices  51.5 us (6%)
  matrix products  50.4 us (6%)
  Pallas kernels  29.9 us (3%)
  other arithmetic  29.3 us (3%)
  between operations  17.7 us (2%)
  loops' own time  10.3 us (1%)
    ppermute x10, waiting for transfers between devices, advance(): inbound = lax.ppermute(output_rows, 'section', RELAY)  433 us
    all_to_all x4, blocking collectives, mixture(): lax.all_to_all(outgoing, 'expert', split_axis=0, concat_axis=0, tiled=True)  90.6 us
    ppermute x3, waiting for transfers between devices, relocated(): return jnp.where(here, value, lax.ppermute(value, 'section', MOVES))  83.9 us
    pallas_call x4, Pallas kernels, expert_rows(): pl.pallas_call(expert_kernel, out_shape=jax.ShapeDtypeStruct((count, mode...  29.9 us
    all_to_all x4, waiting for transfers between devices, mixture(): lax.all_to_all(produced, 'expert', split_axis=0, concat_axis=0, tiled=True)  27.3 us
    unnamed x15, local copies, waits for them, and re-layouts  23 us
    all_to_all x4, starting transfers between devices, mixture(): lax.all_to_all(produced, 'expert', split_axis=0, concat_axis=0, tiled=True)  20.3 us
  transfers between devices with their start and end apart: 23, of which 18 were waited for; matrix products, arithmetic and copies ran while one was open for 10% of the time, Pallas kernels for 0%

profile of v1, /device:TPU:13, one launch (start us, length us, event | category | flops | bytes accessed | tf_op | source)
XLA Modules:
  0.0 908.1 jit_solution(3346677819597860789)
XLA Ops:
  38.2 80.3 %collective-permute-done.1 = f32[2,2048]{1,0:T(2,128)S(1)} collective-permute-done((f32[2,2048]{1,0:T(2,128)S(1)}, f32[2,2048]{1,0:T(2,128)S(1)}, u32[]{:S(2)}, u32[]{:S(2)}) %collective-permute-start.1) | collective-permute-done | bytes 16416 | tf_op jit(solution)/shard_map/ppermute | solution.py:183
  118.8 5.2 all-gather.2.cloned.1.call-done
  128.7 6.5 copy.41
  167.8 720.6 %while.23 = (s32[]{:T(128)}, bf16[32,2048]{1,0:T(8,128)(2,1)S(1)}, bf16[128,128]{1,0:T(8,128)(2,1)}, bf16[128,128]{1,0:T(8,128)(2,1)}, bf16[11,32,2048]{2,1,0:T(...) while((s32[]{:T(128)}, bf16[32,2048]{1,0:T(8,128)(2,1)S(1)}, ...), condition=%wide.region_15.16_spmd.clone.clone, body=%wide.region_9.15_spmd.clone.clone.sunk | while | flops 2611786240 | bytes 43014156 | solution.py:316
  173.6 13.5 %collective-permute-done = bf16[32,2048]{1,0:T(8,128)(2,1)S(1)} collective-permute-done((bf16[32,2048]{1,0:T(8,128)(2,1)}, bf16[32,2048]{1,0:T(8,128)(2,1)S(1)}, u32[]{:S(2)}, u32[]{:S(2)}) %collective-permute-start) | collective-permute-done | bytes 131104 | tf_op jit(solution)/shard_map/while/body/eval_jaxpr/ppermute | solution.py:313
  193.0 6.1 collective-permute-done
  204.9 6.1 collective-permute-done
  216.9 6.1 collective-permute-done
  228.8 6.1 collective-permute-done
  240.8 347.0 %collective-permute-done = bf16[32,2048]{1,0:T(8,128)(2,1)S(1)} collective-permute-done((bf16[32,2048]{1,0:T(8,128)(2,1)}, bf16[32,2048]{1,0:T(8,128)(2,1)S(1)}, u32[]{:S(2)}, u32[]{:S(2)}) %collective-permute-start) | collective-permute-done | bytes 131104 | tf_op jit(solution)/shard_map/while/body/eval_jaxpr/ppermute | solution.py:313
  590.8 59.6 %conditional.8 = (bf16[32,2048]{1,0:T(8,128)(2,1)}, bf16[128,128]{1,0:T(8,128)(2,1)}, bf16[128,128]{1,0:T(8,128)(2,1)}, bf16[1,32,2048]{2,1,0:T(8,128)(2,1)S(1)}) conditional(s32[]{:T(128)} %convert_element_type.264, (bf16[32,2048]{1,0:T(8,128)(2,1)}, bf16[128,128]{1,0:T(8,128)(2,1)}, bf16[128,128]{1,0:T(8,128)(2,1)}) %tuple.121, (s32[]{:T(128)}, ...), branch_computations={%region_10.10_spmd, %region_11.14_spmd} | conditional | flops 2610803200 | bytes 41827776 | solution.py:309
  593.2 24.0 %all_to_all.17 = bf16[32,8,2048]{2,1,0:T(8,128)(2,1)S(1)} all-to-all(bf16[32,8,2048]{2,1,0:T(8,128)(2,1)S(1)} %fusion.45), channel_id=1, replica_groups=mesh['section'=8,'expert'=32] {'expert'}, dimensions={0} | all-to-all | bytes 2097152 | tf_op jit(solution)/shard_map/while/body/eval_jaxpr/cond/branch_1_fun/all_to_all | solution.py:225
  617.2 7.5 experts.3
  624.7 5.1 all-to-all-start.3
  640.4 6.8 all-to-all-done.3
  652.3 15.3 %collective-permute-done = bf16[32,2048]{1,0:T(8,128)(2,1)S(1)} collective-permute-done((bf16[32,2048]{1,0:T(8,128)(2,1)}, bf16[32,2048]{1,0:T(8,128)(2,1)S(1)}, u32[]{:S(2)}, u32[]{:S(2)}) %collective-permute-start) | collective-permute-done | bytes 131104 | tf_op jit(solution)/shard_map/while/body/eval_jaxpr/ppermute | solution.py:313
  670.6 57.7 %conditional.8 = (bf16[32,2048]{1,0:T(8,128)(2,1)}, bf16[128,128]{1,0:T(8,128)(2,1)}, bf16[128,128]{1,0:T(8,128)(2,1)}, bf16[1,32,2048]{2,1,0:T(8,128)(2,1)S(1)}) conditional(s32[]{:T(128)} %convert_element_type.264, (bf16[32,2048]{1,0:T(8,128)(2,1)}, bf16[128,128]{1,0:T(8,128)(2,1)}, bf16[128,128]{1,0:T(8,128)(2,1)}) %tuple.121, (s32[]{:T(128)}, ...), branch_computations={%region_10.10_spmd, %region_11.14_spmd} | conditional | flops 2610803200 | bytes 41827776 | solution.py:309
  673.0 22.2 %all_to_all.17 = bf16[32,8,2048]{2,1,0:T(8,128)(2,1)S(1)} all-to-all(bf16[32,8,2048]{2,1,0:T(8,128)(2,1)S(1)} %fusion.45), channel_id=1, replica_groups=mesh['section'=8,'expert'=32] {'expert'}, dimensions={0} | all-to-all | bytes 2097152 | tf_op jit(solution)/shard_map/while/body/eval_jaxpr/cond/branch_1_fun/all_to_all | solution.py:225
  695.2 7.5 experts.3
  718.3 6.8 all-to-all-done.3
  730.2 9.4 %collective-permute-done = bf16[32,2048]{1,0:T(8,128)(2,1)S(1)} collective-permute-done((bf16[32,2048]{1,0:T(8,128)(2,1)}, bf16[32,2048]{1,0:T(8,128)(2,1)S(1)}, u32[]{:S(2)}, u32[]{:S(2)}) %collective-permute-start) | collective-permute-done | bytes 131104 | tf_op jit(solution)/shard_map/while/body/eval_jaxpr/ppermute | solution.py:313
  742.6 57.7 %conditional.8 = (bf16[32,2048]{1,0:T(8,128)(2,1)}, bf16[128,128]{1,0:T(8,128)(2,1)}, bf16[128,128]{1,0:T(8,128)(2,1)}, bf16[1,32,2048]{2,1,0:T(8,128)(2,1)S(1)}) conditional(s32[]{:T(128)} %convert_element_type.264, (bf16[32,2048]{1,0:T(8,128)(2,1)}, bf16[128,128]{1,0:T(8,128)(2,1)}, bf16[128,128]{1,0:T(8,128)(2,1)}) %tuple.121, (s32[]{:T(128)}, ...), branch_computations={%region_10.10_spmd, %region_11.14_spmd} | conditional | flops 2610803200 | bytes 41827776 | solution.py:309
  745.1 22.2 %all_to_all.17 = bf16[32,8,2048]{2,1,0:T(8,128)(2,1)S(1)} all-to-all(bf16[32,8,2048]{2,1,0:T(8,128)(2,1)S(1)} %fusion.45), channel_id=1, replica_groups=mesh['section'=8,'expert'=32] {'expert'}, dimensions={0} | all-to-all | bytes 2097152 | tf_op jit(solution)/shard_map/while/body/eval_jaxpr/cond/branch_1_fun/all_to_all | solution.py:225
  767.2 7.5 experts.3
  790.4 6.8 all-to-all-done.3
  802.3 17.3 %collective-permute-done = bf16[32,2048]{1,0:T(8,128)(2,1)S(1)} collective-permute-done((bf16[32,2048]{1,0:T(8,128)(2,1)}, bf16[32,2048]{1,0:T(8,128)(2,1)S(1)}, u32[]{:S(2)}, u32[]{:S(2)}) %collective-permute-start) | collective-permute-done | bytes 131104 | tf_op jit(solution)/shard_map/while/body/eval_jaxpr/ppermute | solution.py:313
  822.6 57.7 %conditional.8 = (bf16[32,2048]{1,0:T(8,128)(2,1)}, bf16[128,128]{1,0:T(8,128)(2,1)}, bf16[128,128]{1,0:T(8,128)(2,1)}, bf16[1,32,2048]{2,1,0:T(8,128)(2,1)S(1)}) conditional(s32[]{:T(128)} %convert_element_type.264, (bf16[32,2048]{1,0:T(8,128)(2,1)}, bf16[128,128]{1,0:T(8,128)(2,1)}, bf16[128,128]{1,0:T(8,128)(2,1)}) %tuple.121, (s32[]{:T(128)}, ...), branch_computations={%region_10.10_spmd, %region_11.14_spmd} | conditional | flops 2610803200 | bytes 41827776 | solution.py:309
  825.0 22.2 %all_to_all.17 = bf16[32,8,2048]{2,1,0:T(8,128)(2,1)S(1)} all-to-all(bf16[32,8,2048]{2,1,0:T(8,128)(2,1)S(1)} %fusion.45), channel_id=1, replica_groups=mesh['section'=8,'expert'=32] {'expert'}, dimensions={0} | all-to-all | bytes 2097152 | tf_op jit(solution)/shard_map/while/body/eval_jaxpr/cond/branch_1_fun/all_to_all | solution.py:225
  847.2 7.5 experts.3
  870.3 6.8 all-to-all-done.3
  882.2 6.1 collective-permute-done
  891.4 8.0 collective-permute-done.8
  (180 shorter events, 200.9 us)
Async XLA Ops:
  6.5 112.0 %copy-start.6 = (f32[1,2048]{1,0:T(1,128)S(1)}, f32[1,2048]{1,0:T(1,128)}, u32[]{:S(2)}) copy-start(f32[1,2048]{1,0:T(1,128)} %param.22) | copy-start | bytes 24580
  6.5 112.0 %copy-start.5 = (f32[1,2048]{1,0:T(1,128)S(1)}, f32[1,2048]{1,0:T(1,128)}, u32[]{:S(2)}) copy-start(f32[1,2048]{1,0:T(1,128)} %param.23) | copy-start | bytes 24580
  6.5 117.5 %all-gather.2.cloned.1.call-start = ((), (), s32[]{:S(2)}) async-start(), calls=%async_computation.4 | async-start | bytes 9732096 | tf_op jit(solution)/shard_map/all_gather | solution.py:198
  8.4 7.8 collective-permute-start.2
  18.8 15.2 %collective-permute-start.3 = (s32[4,32,12]{2,1,0:T(8,128)S(1)}, s32[4,32,12]{2,1,0:T(8,128)S(1)}, u32[]{:S(2)}, u32[]{:S(2)}) collective-permute-start(s32[4,32,12]{2,1,0:T(8,128)S(1)} %copy.43), channel_id=1, source_target_pairs={{32,192},{96,128},{128,224},{160,96},{192,32},{224,160},{33,193},{... | collective-permute-start | bytes 18440 | tf_op jit(solution)/shard_map/ppermute | solution.py:183
  20.7 136.4 %collective-permute-start.5 = (bf16[2048,704]{0,1:T(8,128)(2,1)}, bf16[2048,704]{0,1:T(8,128)(2,1)}, u32[]{:S(2)}, u32[]{:S(2)}) collective-permute-start(bf16[2048,704]{0,1:T(8,128)(2,1)} %bitcast.161), channel_id=1, source_target_pairs={{32,192},{96,128},{128,224},{160,96},{192,32},{224,160},{33,193},{... | collective-permute-start | bytes 8650760 | tf_op jit(solution)/shard_map/ppermute | solution.py:206
  24.9 136.8 %collective-permute-start.6 = (bf16[2048,704]{0,1:T(8,128)(2,1)}, bf16[2048,704]{0,1:T(8,128)(2,1)}, u32[]{:S(2)}, u32[]{:S(2)}) collective-permute-start(bf16[2048,704]{0,1:T(8,128)(2,1)} %bitcast.164), channel_id=1, source_target_pairs={{32,192},{96,128},{128,224},{160,96},{192,32},{224,160},{33,193},{... | collective-permute-start | bytes 8650760 | tf_op jit(solution)/shard_map/ppermute | solution.py:206
  27.7 140.0 %collective-permute-start.7 = (bf16[704,2048]{1,0:T(8,128)(2,1)}, bf16[704,2048]{1,0:T(8,128)(2,1)}, u32[]{:S(2)}, u32[]{:S(2)}) collective-permute-start(bf16[704,2048]{1,0:T(8,128)(2,1)} %bitcast.156), channel_id=1, source_target_pairs={{32,192},{96,128},{128,224},{160,96},{192,32},{224,160},{33,193},{... | collective-permute-start | bytes 8650760 | tf_op jit(solution)/shard_map/ppermute | solution.py:206
  32.0 86.5 %collective-permute-start.1 = (f32[2,2048]{1,0:T(2,128)S(1)}, f32[2,2048]{1,0:T(2,128)S(1)}, u32[]{:S(2)}, u32[]{:S(2)}) collective-permute-start(f32[2,2048]{1,0:T(2,128)S(1)} %pad_maximum_fusion), channel_id=1, source_target_pairs={{32,192},{96,128},{128,224},{160,96},{192,32},{224,160},{33,193},{... | collective-permute-start | bytes 49160 | tf_op jit(solution)/shard_map/ppermute | solution.py:183
  141.6 2.7 copy-start.1
  141.6 6.1 copy-start.4
  145.4 22.3 %collective-permute-start.4 = (bf16[32,2048]{1,0:T(8,128)(2,1)S(1)}, bf16[32,2048]{1,0:T(8,128)(2,1)S(1)}, u32[]{:S(2)}, u32[]{:S(2)}) collective-permute-start(bf16[32,2048]{1,0:T(8,128)(2,1)S(1)} %get-tuple-element.607), channel_id=1, source_target_pairs={{0,192},{192,64},{64,128},{128,224},{224,96},{96,32},{32,160},{1,1... | collective-permute-start | bytes 393224 | tf_op jit(solution)/shard_map/ppermute | solution.py:292
  161.7 6.1 copy-start.2
  172.3 14.8 %collective-permute-start = (bf16[32,2048]{1,0:T(8,128)(2,1)}, bf16[32,2048]{1,0:T(8,128)(2,1)S(1)}, u32[]{:S(2)}, u32[]{:S(2)}) collective-permute-start(bf16[32,2048]{1,0:T(8,128)(2,1)} %get-tuple-element.1103), channel_id=1, source_target_pairs={{0,192},{192,64},{64,128},{128,224},{224,96},{96,32},{32,160},{1,1... | collective-permute-start | bytes 393224 | tf_op jit(solution)/shard_map/while/body/eval_jaxpr/ppermute | solution.py:313
  191.7 7.4 collective-permute-start
  203.6 7.4 collective-permute-start
  215.6 7.4 collective-permute-start
  227.5 7.4 collective-permute-start
  239.5 348.3 %collective-permute-start = (bf16[32,2048]{1,0:T(8,128)(2,1)}, bf16[32,2048]{1,0:T(8,128)(2,1)S(1)}, u32[]{:S(2)}, u32[]{:S(2)}) collective-permute-start(bf16[32,2048]{1,0:T(8,128)(2,1)} %get-tuple-element.1103), channel_id=1, source_target_pairs={{0,192},{192,64},{64,128},{128,224},{224,96},{96,32},{32,160},{1,1... | collective-permute-start | bytes 393224 | tf_op jit(solution)/shard_map/while/body/eval_jaxpr/ppermute | solution.py:313
  591.4 25.8 %copy-start.3 = (bf16[2048,704]{1,0:T(8,128)(2,1)S(1)}, bf16[2048,704]{1,0:T(8,128)(2,1)}, u32[]{:S(2)}) copy-start(bf16[2048,704]{1,0:T(8,128)(2,1)} %get-tuple-element.573.gate_own) | copy-start | bytes 8650756 | tf_op jit(solution)/shard_map/while/body/eval_jaxpr/cond
  624.7 22.5 %all-to-all-start.3 = ((bf16[32,8,2048]{2,1,0:T(8,128)(2,1)}), bf16[32,8,2048]{2,1,0:T(8,128)(2,1)}, u32[]{:S(2)}, u32[]{:S(2)}) async-start(bf16[32,8,2048]{2,1,0:T(8,128)(2,1)} %bitcast.26), calls=%async_computation.3 | async-start | bytes 2097152 | tf_op jit(solution)/shard_map/while/body/eval_jaxpr/cond/branch_1_fun/all_to_all | solution.py:228
  651.0 16.6 %collective-permute-start = (bf16[32,2048]{1,0:T(8,128)(2,1)}, bf16[32,2048]{1,0:T(8,128)(2,1)S(1)}, u32[]{:S(2)}, u32[]{:S(2)}) collective-permute-start(bf16[32,2048]{1,0:T(8,128)(2,1)} %get-tuple-element.1103), channel_id=1, source_target_pairs={{0,192},{192,64},{64,128},{128,224},{224,96},{96,32},{32,160},{1,1... | collective-permute-start | bytes 393224 | tf_op jit(solution)/shard_map/while/body/eval_jaxpr/ppermute | solution.py:313
  671.2 23.9 %copy-start.3 = (bf16[2048,704]{1,0:T(8,128)(2,1)S(1)}, bf16[2048,704]{1,0:T(8,128)(2,1)}, u32[]{:S(2)}) copy-start(bf16[2048,704]{1,0:T(8,128)(2,1)} %get-tuple-element.573.gate_own) | copy-start | bytes 8650756 | tf_op jit(solution)/shard_map/while/body/eval_jaxpr/cond
  702.6 22.5 %all-to-all-start.3 = ((bf16[32,8,2048]{2,1,0:T(8,128)(2,1)}), bf16[32,8,2048]{2,1,0:T(8,128)(2,1)}, u32[]{:S(2)}, u32[]{:S(2)}) async-start(bf16[32,8,2048]{2,1,0:T(8,128)(2,1)} %bitcast.26), calls=%async_computation.3 | async-start | bytes 2097152 | tf_op jit(solution)/shard_map/while/body/eval_jaxpr/cond/branch_1_fun/all_to_all | solution.py:228
  728.9 10.7 %collective-permute-start = (bf16[32,2048]{1,0:T(8,128)(2,1)}, bf16[32,2048]{1,0:T(8,128)(2,1)S(1)}, u32[]{:S(2)}, u32[]{:S(2)}) collective-permute-start(bf16[32,2048]{1,0:T(8,128)(2,1)} %get-tuple-element.1103), channel_id=1, source_target_pairs={{0,192},{192,64},{64,128},{128,224},{224,96},{96,32},{32,160},{1,1... | collective-permute-start | bytes 393224 | tf_op jit(solution)/shard_map/while/body/eval_jaxpr/ppermute | solution.py:313
  743.3 23.9 %copy-start.3 = (bf16[2048,704]{1,0:T(8,128)(2,1)S(1)}, bf16[2048,704]{1,0:T(8,128)(2,1)}, u32[]{:S(2)}) copy-start(bf16[2048,704]{1,0:T(8,128)(2,1)} %get-tuple-element.573.gate_own) | copy-start | bytes 8650756 | tf_op jit(solution)/shard_map/while/body/eval_jaxpr/cond
  774.7 22.5 %all-to-all-start.3 = ((bf16[32,8,2048]{2,1,0:T(8,128)(2,1)}), bf16[32,8,2048]{2,1,0:T(8,128)(2,1)}, u32[]{:S(2)}, u32[]{:S(2)}) async-start(bf16[32,8,2048]{2,1,0:T(8,128)(2,1)} %bitcast.26), calls=%async_computation.3 | async-start | bytes 2097152 | tf_op jit(solution)/shard_map/while/body/eval_jaxpr/cond/branch_1_fun/all_to_all | solution.py:228
  801.0 18.6 %collective-permute-start = (bf16[32,2048]{1,0:T(8,128)(2,1)}, bf16[32,2048]{1,0:T(8,128)(2,1)S(1)}, u32[]{:S(2)}, u32[]{:S(2)}) collective-permute-start(bf16[32,2048]{1,0:T(8,128)(2,1)} %get-tuple-element.1103), channel_id=1, source_target_pairs={{0,192},{192,64},{64,128},{128,224},{224,96},{96,32},{32,160},{1,1... | collective-permute-start | bytes 393224 | tf_op jit(solution)/shard_map/while/body/eval_jaxpr/ppermute | solution.py:313
  823.2 23.9 %copy-start.3 = (bf16[2048,704]{1,0:T(8,128)(2,1)S(1)}, bf16[2048,704]{1,0:T(8,128)(2,1)}, u32[]{:S(2)}) copy-start(bf16[2048,704]{1,0:T(8,128)(2,1)} %get-tuple-element.573.gate_own) | copy-start | bytes 8650756 | tf_op jit(solution)/shard_map/while/body/eval_jaxpr/cond
  854.6 22.5 %all-to-all-start.3 = ((bf16[32,8,2048]{2,1,0:T(8,128)(2,1)}), bf16[32,8,2048]{2,1,0:T(8,128)(2,1)}, u32[]{:S(2)}, u32[]{:S(2)}) async-start(bf16[32,8,2048]{2,1,0:T(8,128)(2,1)} %bitcast.26), calls=%async_computation.3 | async-start | bytes 2097152 | tf_op jit(solution)/shard_map/while/body/eval_jaxpr/cond/branch_1_fun/all_to_all | solution.py:228
  880.9 7.4 collective-permute-start
  889.4 9.9 %collective-permute-start.8 = (bf16[4,32,2048]{2,1,0:T(8,128)(2,1)S(1)}, bf16[4,32,2048]{2,1,0:T(8,128)(2,1)S(1)}, u32[]{:S(2)}, u32[]{:S(2)}) collective-permute-start(bf16[4,32,2048]{2,1,0:T(8,128)(2,1)S(1)} %constant_dynamic-slice_fusion), channel_id=1, source_target_pairs={{192,32},{128,96},{224,128},{96,160},{32,192},{160,224},{193,33},{... | collective-permute-start | bytes 1572872 | tf_op jit(solution)/shard_map/ppermute | solution.py:318
Sparse Core Ops, SparseCore 0:
  18.0 105.9 all-gather.1

commit v2 on v1

--- a/solution.py
+++ b/solution.py
@@ -13,124 +13,39 @@
 HOME = [(place, layer) for layer, place in MOVES]
 RELAY = [(POSITION[layer], POSITION[layer + 1]) for layer in range(7)]
 
-CHUNKS = 4
-
-
 def rms_normed(wide, gain_vector):
     scale = lax.rsqrt(jnp.mean(wide * wide, axis=-1, keepdims=True) + epsilon)
     return (wide * scale * gain_vector).astype(jnp.bfloat16)
 
 
-def expert_kernel(
-    moved_ref,
-    rows_ref,
-    gate_own,
-    up_own,
-    down_own,
-    gate_new,
-    up_new,
-    down_new,
-    out_ref,
-    gate_buf,
-    up_buf,
-    down_buf,
-    gate_acc,
-    up_acc,
-    gate_sem,
-    up_sem,
-    down_sem,
-):
-    depth = gate_buf.shape[1]
-    width = down_buf.shape[2]
-
-    def copies(gate_hbm, up_hbm, down_hbm):
-        firsts, lasts = [], []
-        for step in range(CHUNKS):
-            part = pl.ds(step * depth, depth)
-            firsts.append(
-                (
-                    pltpu.make_async_copy(
-                        gate_hbm.at[part, :], gate_buf.at[step], gate_sem.at[step]
-                    ),
-                    pltpu.make_async_copy(up_hbm.at[part, :], up_buf.at[step], up_sem.at[step]),
-                )
-            )
-        for step in range(CHUNKS):
-            part = pl.ds(step * width, width)
-            lasts.append(
-                pltpu.make_async_copy(down_hbm.at[:, part], down_buf.at[step], down_sem.at[step])
-            )
-        return firsts, lasts
-
-    def start(firsts, lasts):
-        for first, second in firsts:
-            first.start()
-            second.start()
-        for copy in lasts:
-            copy.start()
-
-    moved = moved_ref[0]
-
-    @pl.when(moved == 0)
-    def _():
-        start(*copies(gate_own, up_own, down_own))
-
-    @pl.when(moved != 0)
-    def _():
-        start(*copies(gate_new, up_new, down_new))
-
-    firsts, lasts = copies(gate_own, up_own, down_own)
-    for step in range(CHUNKS):
-        first, second = firsts[step]
-        rows = rows_ref[:, step * depth : (step + 1) * depth]
-        first.wait()
-        gated = jnp.dot(rows, gate_buf[step], preferred_element_type=jnp.float32)
-        second.wait()
-        lifted = jnp.dot(rows, up_buf[step], preferred_element_type=jnp.float32)
-        if step == 0:
-            gate_acc[...] = gated
-            up_acc[...] = lifted
-        else:
-            gate_acc[...] += gated
-            up_acc[...] += lifted
-    gated = gate_acc[...]
-    hidden = (gated * jax.nn.sigmoid(gated) * up_acc[...]).astype(jnp.bfloat16)
-    for step in range(CHUNKS):
-        lasts[step].wait()
-        out_ref[:, step * width : (step + 1) * width] = jnp.dot(
-            hidden, down_buf[step], preferred_element_type=jnp.float32
-        ).astype(jnp.bfloat16)
-
-
-def expert_rows(moved, rows, own, new):
+def expert_kernel(rows_ref, gate_ref, up_ref, down_ref, out_ref):
+    rows = rows_ref[...]
+    across = (((1,), (1,)), ((), ()))
+    gated = lax.dot_general(rows, gate_ref[...], across, preferred_element_type=jnp.float32)
+    lifted = lax.dot_general(rows, up_ref[...], across, preferred_element_type=jnp.float32)
+    hidden = (gated * jax.nn.sigmoid(gated) * lifted).astype(jnp.bfloat16)
+    out_ref[...] = jnp.dot(hidden, down_ref[...], preferred_element_type=jnp.float32).astype(
+        jnp.bfloat16
+    )
+
+
+def expert_rows(rows, matrices):
     count, model_width = rows.shape
-    hidden_width = own[0].shape[1]
-    depth = model_width // CHUNKS
+    hidden_width = matrices[2].shape[0]
     vmem = pl.BlockSpec(memory_space=pltpu.VMEM)
-    anywhere = pl.BlockSpec(memory_space=pl.ANY)
     return pl.pallas_call(
         expert_kernel,
         out_shape=jax.ShapeDtypeStruct((count, model_width), jnp.bfloat16),
-        in_specs=[pl.BlockSpec(memory_space=pltpu.SMEM), vmem] + [anywhere] * 6,
+        in_specs=[vmem] * 4,
         out_specs=vmem,
-        scratch_shapes=[
-            pltpu.VMEM((CHUNKS, depth, hidden_width), jnp.bfloat16),
-            pltpu.VMEM((CHUNKS, depth, hidden_width), jnp.bfloat16),
-            pltpu.VMEM((CHUNKS, hidden_width, depth), jnp.bfloat16),
-            pltpu.VMEM((count, hidden_width), jnp.float32),
-            pltpu.VMEM((count, hidden_width), jnp.float32),
-            pltpu.SemaphoreType.DMA((CHUNKS,)),
-            pltpu.SemaphoreType.DMA((CHUNKS,)),
-            pltpu.SemaphoreType.DMA((CHUNKS,)),
-        ],
-        compiler_params=pltpu.CompilerParams(vmem_limit_bytes=40 * 2**20),
+        compiler_params=pltpu.CompilerParams(vmem_limit_bytes=24 * 2**20),
         cost_estimate=pl.CostEstimate(
             flops=6 * count * model_width * hidden_width,
             bytes_accessed=6 * model_width * hidden_width + 4 * count * model_width,
             transcendentals=count * hidden_width,
         ),
         name="experts",
-    )(moved, rows, *own, *new)
+    )(rows, *matrices)
 
 
 def route_tables(picks, codes, expert_count, capacity):
@@ -177,7 +92,6 @@
     capacity = min(tok_rows, tok_rows * pick_count * 4 // (3 * expert_count))
     layer = jnp.asarray(LAYER_AT, jnp.int32)[place]
     here = layer == place
-    moved = (layer != place).astype(jnp.int32).reshape(1)
 
     def relocated(value):
         return jnp.where(here, value, lax.ppermute(value, "section", MOVES))
@@ -202,8 +116,9 @@
     scatter_tables, combine_tables = route_tables(
         tables[:, :, :pick_count], tables[:, :, pick_count:], expert_count, capacity
     )
-    own = (gate_proj[0, 0], up_proj[0, 0], down_proj[0, 0])
-    new = tuple(lax.ppermute(value, "section", MOVES) for value in own)
+    scatter_tables, combine_tables = lax.optimization_barrier((scatter_tables, combine_tables))
+    own = (gate_proj[0, 0].T, up_proj[0, 0].T, down_proj[0, 0])
+    here_matrices = tuple(relocated(value) for value in own)
 
     score_width = (head_count + 2) * head_size
     length = micro_count * tok_rows
@@ -211,11 +126,14 @@
 
     def attention_weights(full):
         rows = out_shard.shape[0]
-        halves = full[:, score_width:].reshape(expert_devices, 2, rows, half)
-        halves = halves.transpose(0, 2, 1, 3).reshape(expert_devices * rows, model_width)
-        return (full[:, :score_width], halves)
-
-    def mixture(layer_input, block, own, new, moved):
+        halves = full.reshape(expert_devices, 2, rows, score_width + half)
+        outer = tuple(
+            halves[:, side, :, score_width:].reshape(expert_devices * rows, half)
+            for side in range(2)
+        )
+        return (full[:, :score_width], outer)
+
+    def mixture(layer_input, block, matrices):
         wide = layer_input.astype(jnp.float32)
         normed = rms_normed(wide, moe_gain)
         scatter_table = lax.dynamic_index_in_dim(scatter_tables, block, 0, keepdims=False)
@@ -223,7 +141,7 @@
         outgoing = jnp.einsum("te,td->ed", scatter_table, normed, preferred_element_type=jnp.float32)
         outgoing = outgoing.astype(jnp.bfloat16).reshape(expert_count, capacity, model_width)
         arrived = lax.all_to_all(outgoing, "expert", split_axis=0, concat_axis=0, tiled=True)
-        produced = expert_rows(moved, arrived.reshape(-1, model_width), own, new)
+        produced = expert_rows(arrived.reshape(-1, model_width), matrices)
         produced = produced.reshape(arrived.shape)
         returned = lax.all_to_all(produced, "expert", split_axis=0, concat_axis=0, tiled=True)
         return jnp.dot(
@@ -258,7 +176,9 @@
             preferred_element_type=jnp.float32,
         )
         context = context.astype(jnp.bfloat16).reshape(tok_rows, head_count * head_size)
-        attended = jnp.dot(context, outer, preferred_element_type=jnp.float32)
+        attended = jnp.concatenate(
+            [jnp.dot(context, side, preferred_element_type=jnp.float32) for side in outer], axis=1
+        )
         return (attended, key_vectors, value_vectors)
 
     keys = jnp.zeros((length, head_size), jnp.bfloat16)
@@ -268,10 +188,11 @@
     first_rows = tokens[0]
     mixed = lax.cond(
         leading,
-        lambda rows: mixture(rows, first_block, own, own, jnp.zeros((1,), jnp.int32)),
+        lambda rows: mixture(rows, first_block, own),
         lambda rows: jnp.zeros((tok_rows, model_width), jnp.float32),
         first_rows,
     )
+    full, here_matrices = lax.optimization_barrier((full, here_matrices))
     inner, outer = attention_weights(full)
 
     def first_attend(arrays):
@@ -289,10 +210,10 @@
     tick_count = micro_count + section_count - 1
     stored = jnp.zeros((tick_count, tok_rows, model_width), jnp.bfloat16)
     stored = lax.dynamic_update_index_in_dim(stored, output_rows, 0, 0)
-    inbound = lax.ppermute(output_rows, "section", RELAY)
 
     def advance(tick_index, state_carry):
-        inbound, keys, values, stored = state_carry
+        output_rows, keys, values, stored = state_carry
+        inbound = lax.ppermute(output_rows, "section", RELAY)
         block_index = tick_index - layer
         active = (block_index >= 0) & (block_index < micro_count)
         block = jnp.clip(block_index, 0, micro_count - 1)
@@ -301,7 +222,7 @@
             inbound, keys, values = arrays
             held = lax.dynamic_index_in_dim(tokens, block, 0, keepdims=False)
             layer_input = jnp.where(layer == 0, held, inbound)
-            mixed = mixture(layer_input, block, own, new, moved)
+            mixed = mixture(layer_input, block, here_matrices)
             attended, keys, values = attend(layer_input, block, keys, values, inner, outer)
             output_rows = layer_input.astype(jnp.float32) + attended + mixed
             return (output_rows.astype(jnp.bfloat16), keys, values)
@@ -310,10 +231,9 @@
             active, work, lambda arrays: arrays, (inbound, keys, values)
         )
         stored = lax.dynamic_update_index_in_dim(stored, output_rows, tick_index, 0)
-        inbound = lax.ppermute(output_rows, "section", RELAY)
-        return (inbound, keys, values, stored)
-
-    finals = lax.fori_loop(1, tick_count, advance, (inbound, keys, values, stored))
+        return (output_rows, keys, values, stored)
+
+    finals = lax.fori_loop(1, tick_count, advance, (output_rows, keys, values, stored))
     results = lax.dynamic_slice_in_dim(finals[3], layer, micro_count, 0)
     returned_home = lax.ppermute(results, "section", HOME)
     return jnp.where(here, results, returned_home)[None]

time: 914 us -> 863 us (0.944)
  local copies, waits for them, and re-layouts: 70.8 us -> 48.6 us
  waiting for transfers between devices: 558 us -> 545 us
    unnamed x15 -> x16, local copies, waits for them, and re-layouts: 23 us -> 0.04 us
    convert_element_type x10 -> x0, other arithmetic: 16.3 us -> none  [route_tables(): scatter_table.astype(jnp.bfloat16)]
    select_n x3 -> x6, other arithmetic: 1.75 us -> 13.4 us  [relocated(): return jnp.where(here, value, lax.ppermute(value, 'section', MOVES))]
    ppermute x4 -> x0, starting transfers between devices: 10.5 us -> none  [the longest x3 8.97 us: shards(): new = tuple((lax.ppermute(value, 'section', MOVES) for value in own))]
    ppermute x3 -> x6, waiting for transfers between devices: 83.9 us -> 75.3 us  [relocated(): return jnp.where(here, value, lax.ppermute(value, 'section', MOVES))]
  transfers between devices with their start and end apart: 23 -> 22, of which waited for: 18 -> 19; matrix products, arithmetic and copies ran while one was open for 10% -> 7% of each run, Pallas kernels for 0% -> 0%
where the time goes in v2:
time: 863 us; the launch traced here: 859 us
  waiting for transfers between devices  545 us (63%)
  blocking collectives  88.7 us (10%)
  starting transfers between devices  49.7 us (6%)
  matrix products  49.7 us (6%)
  local copies, waits for them, and re-layouts  48.6 us (6%)
  Pallas kernels  28.8 us (3%)
  other arithmetic  23.8 us (3%)
  between operations  16.4 us (2%)
    ppermute x10, waiting for transfers between devices, advance(): inbound = lax.ppermute(output_rows, 'section', RELAY)  434 us
    all_to_all x4, blocking collectives, mixture(): lax.all_to_all(outgoing, 'expert', split_axis=0, concat_axis=0, tiled=True)  88.7 us
    ppermute x6, waiting for transfers between devices, relocated(): return jnp.where(here, value, lax.ppermute(value, 'section', MOVES))  75.3 us
    pallas_call x4, Pallas kernels, expert_rows(): pl.pallas_call(expert_kernel, out_shape=jax.ShapeDtypeStruct((count, mode...  28.8 us
    all_to_all x4, waiting for transfers between devices, mixture(): lax.all_to_all(produced, 'expert', split_axis=0, concat_axis=0, tiled=True)  24 us
    all_to_all x4, starting transfers between devices, mixture(): lax.all_to_all(produced, 'expert', split_axis=0, concat_axis=0, tiled=True)  20 us
  transfers between devices with their start and end apart: 22, of which 19 were waited for; matrix products, arithmetic and copies ran while one was open for 7% of the time, Pallas kernels for 0%

profile of v2, /device:TPU:13, one launch (start us, length us, event | category | flops | bytes accessed | tf_op | source)
XLA Modules:
  0.0 859.3 jit_solution(10055156221863613448)
XLA Ops:
  35.9 50.8 %collective-permute-done.6 = s32[4,32,12]{2,1,0:T(8,128)S(1)} collective-permute-done((s32[4,32,12]{2,1,0:T(8,128)S(1)}, s32[4,32,12]{2,1,0:T(8,128)S(1)}, u32[]{:S(2)}, u32[]{:S(2)}) %collective-permute-start.6) | collective-permute-done | bytes 6176 | tf_op jit(solution)/shard_map/ppermute | solution.py:97
  97.0 20.5 %collective-permute-done.5 = bf16[704,2048]{1,0:T(8,128)(2,1)} collective-permute-done((bf16[704,2048]{1,0:T(8,128)(2,1)}, bf16[704,2048]{1,0:T(8,128)(2,1)}, u32[]{:S(2)}, u32[]{:S(2)}) %collective-permute-start.5) | collective-permute-done | bytes 2883616 | tf_op jit(solution)/shard_map/ppermute | solution.py:97
  128.7 6.1 fusion.105
  137.3 702.3 %while.21 = (s32[]{:T(128)}, bf16[32,2048]{1,0:T(8,128)(2,1)S(1)}, bf16[128,128]{1,0:T(8,128)(2,1)}, bf16[128,128]{1,0:T(8,128)(2,1)}, bf16[11,32,2048]{2,1,0:T(...) while((s32[]{:T(128)}, bf16[32,2048]{1,0:T(8,128)(2,1)S(1)}, ...), condition=%wide.region_15.16_spmd, body=%wide.region_9.15_spmd.sunk | while | flops 2610868480 | bytes 39796268 | solution.py:236
  139.2 12.1 %collective-permute-done = bf16[32,2048]{1,0:T(8,128)(2,1)} collective-permute-done((bf16[32,2048]{1,0:T(8,128)(2,1)S(1)}, bf16[32,2048]{1,0:T(8,128)(2,1)}, u32[]{:S(2)}, u32[]{:S(2)}) %collective-permute-start) | collective-permute-done | bytes 131104 | tf_op jit(solution)/shard_map/while/body/eval_jaxpr/ppermute | solution.py:216
  155.6 5.5 collective-permute-done
  165.4 5.5 collective-permute-done
  175.2 5.5 collective-permute-done
  185.0 5.5 collective-permute-done
  194.8 5.5 collective-permute-done
  204.5 373.4 %collective-permute-done = bf16[32,2048]{1,0:T(8,128)(2,1)} collective-permute-done((bf16[32,2048]{1,0:T(8,128)(2,1)S(1)}, bf16[32,2048]{1,0:T(8,128)(2,1)}, u32[]{:S(2)}, u32[]{:S(2)}) %collective-permute-start) | collective-permute-done | bytes 131104 | tf_op jit(solution)/shard_map/while/body/eval_jaxpr/ppermute | solution.py:216
  578.0 57.3 %conditional.6 = (bf16[32,2048]{1,0:T(8,128)(2,1)}, bf16[128,128]{1,0:T(8,128)(2,1)}, bf16[128,128]{1,0:T(8,128)(2,1)}, bf16[1,32,2048]{2,1,0:T(8,128)(2,1)S(1)}) conditional(s32[]{:T(128)} %convert_element_type.205, (bf16[32,2048]{1,0:T(8,128)(2,1)}, bf16[128,128]{1,0:T(8,128)(2,1)}, bf16[128,128]{1,0:T(8,128)(2,1)}) %tuple.100, (s32[]{:T(128)}, ...), branch_computations={%region_10.10_spmd, %region_11.14_spmd} | conditional | flops 2610868480 | bytes 38747228 | solution.py:230
  580.9 22.2 %all_to_all.18 = bf16[32,8,2048]{2,1,0:T(8,128)(2,1)S(1)} all-to-all(bf16[32,8,2048]{2,1,0:T(8,128)(2,1)S(1)} %fusion.45), channel_id=1, replica_groups=mesh['section'=8,'expert'=32] {'expert'}, dimensions={0} | all-to-all | bytes 2097152 | tf_op jit(solution)/shard_map/while/body/eval_jaxpr/cond/branch_1_fun/all_to_all | solution.py:143
  603.1 7.2 experts.3
  610.3 5.0 all-to-all-start.3
  626.7 6.0 all-to-all-done.3
  638.6 5.5 collective-permute-done
  644.1 57.3 %conditional.6 = (bf16[32,2048]{1,0:T(8,128)(2,1)}, bf16[128,128]{1,0:T(8,128)(2,1)}, bf16[128,128]{1,0:T(8,128)(2,1)}, bf16[1,32,2048]{2,1,0:T(8,128)(2,1)S(1)}) conditional(s32[]{:T(128)} %convert_element_type.205, (bf16[32,2048]{1,0:T(8,128)(2,1)}, bf16[128,128]{1,0:T(8,128)(2,1)}, bf16[128,128]{1,0:T(8,128)(2,1)}) %tuple.100, (s32[]{:T(128)}, ...), branch_computations={%region_10.10_spmd, %region_11.14_spmd} | conditional | flops 2610868480 | bytes 38747228 | solution.py:230
  647.0 22.2 %all_to_all.18 = bf16[32,8,2048]{2,1,0:T(8,128)(2,1)S(1)} all-to-all(bf16[32,8,2048]{2,1,0:T(8,128)(2,1)S(1)} %fusion.45), channel_id=1, replica_groups=mesh['section'=8,'expert'=32] {'expert'}, dimensions={0} | all-to-all | bytes 2097152 | tf_op jit(solution)/shard_map/while/body/eval_jaxpr/cond/branch_1_fun/all_to_all | solution.py:143
  669.2 7.2 experts.3
  692.8 6.0 all-to-all-done.3
  704.8 5.5 collective-permute-done
  710.2 57.3 %conditional.6 = (bf16[32,2048]{1,0:T(8,128)(2,1)}, bf16[128,128]{1,0:T(8,128)(2,1)}, bf16[128,128]{1,0:T(8,128)(2,1)}, bf16[1,32,2048]{2,1,0:T(8,128)(2,1)S(1)}) conditional(s32[]{:T(128)} %convert_element_type.205, (bf16[32,2048]{1,0:T(8,128)(2,1)}, bf16[128,128]{1,0:T(8,128)(2,1)}, bf16[128,128]{1,0:T(8,128)(2,1)}) %tuple.100, (s32[]{:T(128)}, ...), branch_computations={%region_10.10_spmd, %region_11.14_spmd} | conditional | flops 2610868480 | bytes 38747228 | solution.py:230
  713.2 22.2 %all_to_all.18 = bf16[32,8,2048]{2,1,0:T(8,128)(2,1)S(1)} all-to-all(bf16[32,8,2048]{2,1,0:T(8,128)(2,1)S(1)} %fusion.45), channel_id=1, replica_groups=mesh['section'=8,'expert'=32] {'expert'}, dimensions={0} | all-to-all | bytes 2097152 | tf_op jit(solution)/shard_map/while/body/eval_jaxpr/cond/branch_1_fun/all_to_all | solution.py:143
  735.3 7.2 experts.3
  759.0 6.0 all-to-all-done.3
  770.9 9.8 %collective-permute-done = bf16[32,2048]{1,0:T(8,128)(2,1)} collective-permute-done((bf16[32,2048]{1,0:T(8,128)(2,1)S(1)}, bf16[32,2048]{1,0:T(8,128)(2,1)}, u32[]{:S(2)}, u32[]{:S(2)}) %collective-permute-start) | collective-permute-done | bytes 131104 | tf_op jit(solution)/shard_map/while/body/eval_jaxpr/ppermute | solution.py:216
  780.7 57.3 %conditional.6 = (bf16[32,2048]{1,0:T(8,128)(2,1)}, bf16[128,128]{1,0:T(8,128)(2,1)}, bf16[128,128]{1,0:T(8,128)(2,1)}, bf16[1,32,2048]{2,1,0:T(8,128)(2,1)S(1)}) conditional(s32[]{:T(128)} %convert_element_type.205, (bf16[32,2048]{1,0:T(8,128)(2,1)}, bf16[128,128]{1,0:T(8,128)(2,1)}, bf16[128,128]{1,0:T(8,128)(2,1)}) %tuple.100, (s32[]{:T(128)}, ...), branch_computations={%region_10.10_spmd, %region_11.14_spmd} | conditional | flops 2610868480 | bytes 38747228 | solution.py:230
  783.7 22.2 %all_to_all.18 = bf16[32,8,2048]{2,1,0:T(8,128)(2,1)S(1)} all-to-all(bf16[32,8,2048]{2,1,0:T(8,128)(2,1)S(1)} %fusion.45), channel_id=1, replica_groups=mesh['section'=8,'expert'=32] {'expert'}, dimensions={0} | all-to-all | bytes 2097152 | tf_op jit(solution)/shard_map/while/body/eval_jaxpr/cond/branch_1_fun/all_to_all | solution.py:143
  805.8 7.2 experts.3
  829.5 6.0 all-to-all-done.3
  842.6 8.0 collective-permute-done.7
  (179 shorter events, 175.8 us)
Async XLA Ops:
  6.5 22.2 %copy-start.10 = (s32[1,4,32,6]{2,1,3,0:T(4,128)S(1)}, s32[1,4,32,6]{2,1,3,0:T(4,128)}, u32[]{:S(2)}) copy-start(s32[1,4,32,6]{2,1,3,0:T(4,128)} %param.32) | copy-start | bytes 9220
  6.5 22.2 %copy-start.11 = (s32[1,4,32,6]{2,1,3,0:T(4,128)S(1)}, s32[1,4,32,6]{2,1,3,0:T(4,128)}, u32[]{:S(2)}) copy-start(s32[1,4,32,6]{2,1,3,0:T(4,128)} %param.31) | copy-start | bytes 9220
  6.5 119.3 %all-gather.2.cloned.1.call-start = ((), (), s32[]{:S(2)}) async-start(), calls=%async_computation.4 | async-start | bytes 9732096 | tf_op jit(solution)/shard_map/all_gather | solution.py:112
  7.4 81.6 %copy-start.8 = (f32[1,2048]{1,0:T(1,128)S(1)}, f32[1,2048]{1,0:T(1,128)}, u32[]{:S(2)}) copy-start(f32[1,2048]{1,0:T(1,128)} %param.23) | copy-start | bytes 24580
  7.5 81.6 %copy-start.9 = (f32[1,2048]{1,0:T(1,128)S(1)}, f32[1,2048]{1,0:T(1,128)}, u32[]{:S(2)}) copy-start(f32[1,2048]{1,0:T(1,128)} %param.22) | copy-start | bytes 24580
  7.5 81.7 %copy-start.3 = (bf16[1,1,2048,704]{2,3,1,0:T(8,128)(2,1)S(1)}, bf16[1,1,2048,704]{2,3,1,0:T(8,128)(2,1)}, u32[]{:S(2)}) copy-start(bf16[1,1,2048,704]{2,3,1,0:T(8,128)(2,1)} %param.28) | copy-start | bytes 8650756
  9.3 8.0 collective-permute-start.2
  19.0 70.2 %collective-permute-start.3 = (bf16[704,2048]{1,0:T(8,128)(2,1)}, bf16[704,2048]{1,0:T(8,128)(2,1)}, u32[]{:S(2)}, u32[]{:S(2)}) collective-permute-start(bf16[704,2048]{1,0:T(8,128)(2,1)} %bitcast.173), channel_id=1, source_target_pairs={{32,192},{96,128},{128,224},{160,96},{192,32},{224,160},{33,193},{... | collective-permute-start | bytes 8650760 | tf_op jit(solution)/shard_map/ppermute | solution.py:97
  21.7 67.4 %collective-permute-start.1 = (f32[2,2048]{1,0:T(2,128)S(1)}, f32[2,2048]{1,0:T(2,128)S(1)}, u32[]{:S(2)}, u32[]{:S(2)}) collective-permute-start(f32[2,2048]{1,0:T(2,128)S(1)} %pad_maximum_fusion), channel_id=1, source_target_pairs={{32,192},{96,128},{128,224},{160,96},{192,32},{224,160},{33,193},{... | collective-permute-start | bytes 49160 | tf_op jit(solution)/shard_map/ppermute | solution.py:97
  25.9 67.2 %collective-permute-start.4 = (bf16[704,2048]{1,0:T(8,128)(2,1)}, bf16[704,2048]{1,0:T(8,128)(2,1)}, u32[]{:S(2)}, u32[]{:S(2)}) collective-permute-start(bf16[704,2048]{1,0:T(8,128)(2,1)} %bitcast.175), channel_id=1, source_target_pairs={{32,192},{96,128},{128,224},{160,96},{192,32},{224,160},{33,193},{... | collective-permute-start | bytes 8650760 | tf_op jit(solution)/shard_map/ppermute | solution.py:97
  28.9 57.8 %collective-permute-start.6 = (s32[4,32,12]{2,1,0:T(8,128)S(1)}, s32[4,32,12]{2,1,0:T(8,128)S(1)}, u32[]{:S(2)}, u32[]{:S(2)}) collective-permute-start(s32[4,32,12]{2,1,0:T(8,128)S(1)} %copy.41), channel_id=1, source_target_pairs={{32,192},{96,128},{128,224},{160,96},{192,32},{224,160},{33,193},{... | collective-permute-start | bytes 18440 | tf_op jit(solution)/shard_map/ppermute | solution.py:97
  34.0 83.6 %collective-permute-start.5 = (bf16[704,2048]{1,0:T(8,128)(2,1)}, bf16[704,2048]{1,0:T(8,128)(2,1)}, u32[]{:S(2)}, u32[]{:S(2)}) collective-permute-start(bf16[704,2048]{1,0:T(8,128)(2,1)} %bitcast.177), channel_id=1, source_target_pairs={{32,192},{96,128},{128,224},{160,96},{192,32},{224,160},{33,193},{... | collective-permute-start | bytes 8650760 | tf_op jit(solution)/shard_map/ppermute | solution.py:97
  89.2 3.9 copy-start.4
  93.1 24.5 %copy-start.6 = (bf16[1,1,704,2048]{3,2,1,0:T(8,128)(2,1)S(1)}, bf16[1,1,704,2048]{3,2,1,0:T(8,128)(2,1)}, u32[]{:S(2)}) copy-start(bf16[1,1,704,2048]{3,2,1,0:T(8,128)(2,1)} %param.30) | copy-start | bytes 8650756
  128.7 6.1 copy-start
  137.3 14.0 %collective-permute-start = (bf16[32,2048]{1,0:T(8,128)(2,1)S(1)}, bf16[32,2048]{1,0:T(8,128)(2,1)}, u32[]{:S(2)}, u32[]{:S(2)}) collective-permute-start(bf16[32,2048]{1,0:T(8,128)(2,1)S(1)} %get-tuple-element.765), channel_id=1, source_target_pairs={{0,192},{192,64},{64,128},{128,224},{224,96},{96,32},{32,160},{1,1... | collective-permute-start | bytes 393224 | tf_op jit(solution)/shard_map/while/body/eval_jaxpr/ppermute | solution.py:216
  153.8 7.3 collective-permute-start
  163.5 7.3 collective-permute-start
  173.3 7.3 collective-permute-start
  183.1 7.3 collective-permute-start
  192.9 7.3 collective-permute-start
  202.7 375.3 %collective-permute-start = (bf16[32,2048]{1,0:T(8,128)(2,1)S(1)}, bf16[32,2048]{1,0:T(8,128)(2,1)}, u32[]{:S(2)}, u32[]{:S(2)}) collective-permute-start(bf16[32,2048]{1,0:T(8,128)(2,1)S(1)} %get-tuple-element.765), channel_id=1, source_target_pairs={{0,192},{192,64},{64,128},{128,224},{224,96},{96,32},{32,160},{1,1... | collective-permute-start | bytes 393224 | tf_op jit(solution)/shard_map/while/body/eval_jaxpr/ppermute | solution.py:216
  610.3 22.4 %all-to-all-start.3 = ((bf16[32,8,2048]{2,1,0:T(8,128)(2,1)}), bf16[32,8,2048]{2,1,0:T(8,128)(2,1)S(1)}, u32[]{:S(2)}, u32[]{:S(2)}) async-start(bf16[32,8,2048]{2,1,0:T(8,128)(2,1)} %bitcast.26), calls=%async_computation.3 | async-start | bytes 2097152 | tf_op jit(solution)/shard_map/while/body/eval_jaxpr/cond/branch_1_fun/all_to_all | solution.py:146
  623.7 1.6 copy-start.2
  636.8 7.3 collective-permute-start
  676.4 22.4 %all-to-all-start.3 = ((bf16[32,8,2048]{2,1,0:T(8,128)(2,1)}), bf16[32,8,2048]{2,1,0:T(8,128)(2,1)S(1)}, u32[]{:S(2)}, u32[]{:S(2)}) async-start(bf16[32,8,2048]{2,1,0:T(8,128)(2,1)} %bitcast.26), calls=%async_computation.3 | async-start | bytes 2097152 | tf_op jit(solution)/shard_map/while/body/eval_jaxpr/cond/branch_1_fun/all_to_all | solution.py:146
  702.9 7.3 collective-permute-start
  742.6 22.4 %all-to-all-start.3 = ((bf16[32,8,2048]{2,1,0:T(8,128)(2,1)}), bf16[32,8,2048]{2,1,0:T(8,128)(2,1)S(1)}, u32[]{:S(2)}, u32[]{:S(2)}) async-start(bf16[32,8,2048]{2,1,0:T(8,128)(2,1)} %bitcast.26), calls=%async_computation.3 | async-start | bytes 2097152 | tf_op jit(solution)/shard_map/while/body/eval_jaxpr/cond/branch_1_fun/all_to_all | solution.py:146
  756.0 1.6 copy-start.2
  769.1 11.7 %collective-permute-start = (bf16[32,2048]{1,0:T(8,128)(2,1)S(1)}, bf16[32,2048]{1,0:T(8,128)(2,1)}, u32[]{:S(2)}, u32[]{:S(2)}) collective-permute-start(bf16[32,2048]{1,0:T(8,128)(2,1)S(1)} %get-tuple-element.765), channel_id=1, source_target_pairs={{0,192},{192,64},{64,128},{128,224},{224,96},{96,32},{32,160},{1,1... | collective-permute-start | bytes 393224 | tf_op jit(solution)/shard_map/while/body/eval_jaxpr/ppermute | solution.py:216
  813.1 22.4 %all-to-all-start.3 = ((bf16[32,8,2048]{2,1,0:T(8,128)(2,1)}), bf16[32,8,2048]{2,1,0:T(8,128)(2,1)S(1)}, u32[]{:S(2)}, u32[]{:S(2)}) async-start(bf16[32,8,2048]{2,1,0:T(8,128)(2,1)} %bitcast.26), calls=%async_computation.3 | async-start | bytes 2097152 | tf_op jit(solution)/shard_map/while/body/eval_jaxpr/cond/branch_1_fun/all_to_all | solution.py:146
  840.6 9.9 %collective-permute-start.7 = (bf16[4,32,2048]{2,1,0:T(8,128)(2,1)S(1)}, bf16[4,32,2048]{2,1,0:T(8,128)(2,1)S(1)}, u32[]{:S(2)}, u32[]{:S(2)}) collective-permute-start(bf16[4,32,2048]{2,1,0:T(8,128)(2,1)S(1)} %constant_dynamic-slice_fusion), channel_id=1, source_target_pairs={{192,32},{128,96},{224,128},{96,160},{32,192},{160,224},{193,33},{... | collective-permute-start | bytes 1572872 | tf_op jit(solution)/shard_map/ppermute | solution.py:238
  (6 other events, 5.8 us)
Sparse Core Ops, SparseCore 0:
  19.1 106.6 all-gather.1

commit v3 on v2

--- a/solution.py
+++ b/solution.py
@@ -13,31 +13,76 @@
 HOME = [(place, layer) for layer, place in MOVES]
 RELAY = [(POSITION[layer], POSITION[layer + 1]) for layer in range(7)]
 
+SPAN = 352
+FLIGHT = 3
+
+
 def rms_normed(wide, gain_vector):
     scale = lax.rsqrt(jnp.mean(wide * wide, axis=-1, keepdims=True) + epsilon)
     return (wide * scale * gain_vector).astype(jnp.bfloat16)
 
 
-def expert_kernel(rows_ref, gate_ref, up_ref, down_ref, out_ref):
+def expert_kernel(
+    rows_ref, gate_hbm, up_hbm, down_hbm, out_ref, gate_buf, up_buf, down_buf, hidden_buf, sems
+):
+    hidden_width = down_buf.shape[0]
+    spans = [
+        pl.ds(first, min(SPAN, hidden_width - first)) for first in range(0, hidden_width, SPAN)
+    ]
+    sources = []
+    for span in spans:
+        sources.append((gate_hbm, gate_buf, span))
+        sources.append((up_hbm, up_buf, span))
+    for span in spans:
+        sources.append((down_hbm, down_buf, span))
+    copies = [
+        pltpu.make_async_copy(source.at[span, :], target.at[span, :], sems.at[number])
+        for number, (source, target, span) in enumerate(sources)
+    ]
+    for copy in copies[:FLIGHT]:
+        copy.start()
+
+    def arrive(number):
+        copies[number].wait()
+        if number + FLIGHT < len(copies):
+            copies[number + FLIGHT].start()
+
+    across = (((1,), (1,)), ((), ()))
     rows = rows_ref[...]
-    across = (((1,), (1,)), ((), ()))
-    gated = lax.dot_general(rows, gate_ref[...], across, preferred_element_type=jnp.float32)
-    lifted = lax.dot_general(rows, up_ref[...], across, preferred_element_type=jnp.float32)
-    hidden = (gated * jax.nn.sigmoid(gated) * lifted).astype(jnp.bfloat16)
-    out_ref[...] = jnp.dot(hidden, down_ref[...], preferred_element_type=jnp.float32).astype(
-        jnp.bfloat16
-    )
+    for number, span in enumerate(spans):
+        arrive(2 * number)
+        gated = lax.dot_general(
+            rows, gate_buf[span, :], across, preferred_element_type=jnp.float32
+        )
+        arrive(2 * number + 1)
+        lifted = lax.dot_general(rows, up_buf[span, :], across, preferred_element_type=jnp.float32)
+        hidden = gated * jax.nn.sigmoid(gated) * lifted
+        hidden_buf[:, span] = hidden.astype(jnp.bfloat16)
+    for number in range(len(spans)):
+        arrive(2 * len(spans) + number)
+    out_ref[...] = jnp.dot(
+        hidden_buf[...], down_buf[...], preferred_element_type=jnp.float32
+    ).astype(jnp.bfloat16)
 
 
 def expert_rows(rows, matrices):
     count, model_width = rows.shape
     hidden_width = matrices[2].shape[0]
     vmem = pl.BlockSpec(memory_space=pltpu.VMEM)
+    anywhere = pl.BlockSpec(memory_space=pl.ANY)
+    copy_count = 3 * -(-hidden_width // SPAN)
     return pl.pallas_call(
         expert_kernel,
         out_shape=jax.ShapeDtypeStruct((count, model_width), jnp.bfloat16),
-        in_specs=[vmem] * 4,
+        in_specs=[vmem, anywhere, anywhere, anywhere],
         out_specs=vmem,
+        scratch_shapes=[
+            pltpu.VMEM((hidden_width, model_width), jnp.bfloat16),
+            pltpu.VMEM((hidden_width, model_width), jnp.bfloat16),
+            pltpu.VMEM((hidden_width, model_width), jnp.bfloat16),
+            pltpu.VMEM((count, hidden_width), jnp.bfloat16),
+            pltpu.SemaphoreType.DMA((copy_count,)),
+        ],
         compiler_params=pltpu.CompilerParams(vmem_limit_bytes=24 * 2**20),
         cost_estimate=pl.CostEstimate(
             flops=6 * count * model_width * hidden_width,
@@ -198,22 +243,23 @@
     def first_attend(arrays):
         rows, mixed, keys, values = arrays
         attended, keys, values = attend(rows, first_block, keys, values, inner, outer)
-        output_rows = (rows.astype(jnp.float32) + attended + mixed).astype(jnp.bfloat16)
-        return (output_rows, keys, values)
-
-    output_rows, keys, values = lax.cond(
+        return (rows.astype(jnp.float32) + attended + mixed, keys, values)
+
+    nothing = jnp.zeros((tok_rows, model_width), jnp.float32)
+    total, keys, values = lax.cond(
         leading,
         first_attend,
-        lambda arrays: (arrays[0], arrays[2], arrays[3]),
+        lambda arrays: (nothing, arrays[2], arrays[3]),
         (first_rows, mixed, keys, values),
     )
     tick_count = micro_count + section_count - 1
     stored = jnp.zeros((tick_count, tok_rows, model_width), jnp.bfloat16)
-    stored = lax.dynamic_update_index_in_dim(stored, output_rows, 0, 0)
+    output_rows = total.astype(jnp.bfloat16)
 
     def advance(tick_index, state_carry):
         output_rows, keys, values, stored = state_carry
         inbound = lax.ppermute(output_rows, "section", RELAY)
+        stored = lax.dynamic_update_index_in_dim(stored, output_rows, tick_index - 1, 0)
         block_index = tick_index - layer
         active = (block_index >= 0) & (block_index < micro_count)
         block = jnp.clip(block_index, 0, micro_count - 1)
@@ -225,16 +271,16 @@
             mixed = mixture(layer_input, block, here_matrices)
             attended, keys, values = attend(layer_input, block, keys, values, inner, outer)
             output_rows = layer_input.astype(jnp.float32) + attended + mixed
-            return (output_rows.astype(jnp.bfloat16), keys, values)
-
-        output_rows, keys, values = lax.cond(
-            active, work, lambda arrays: arrays, (inbound, keys, values)
-        )
-        stored = lax.dynamic_update_index_in_dim(stored, output_rows, tick_index, 0)
-        return (output_rows, keys, values, stored)
+            return (output_rows, keys, values)
+
+        total, keys, values = lax.cond(
+            active, work, lambda arrays: (nothing, *arrays[1:]), (inbound, keys, values)
+        )
+        return (total.astype(jnp.bfloat16), keys, values, stored)
 
     finals = lax.fori_loop(1, tick_count, advance, (output_rows, keys, values, stored))
-    results = lax.dynamic_slice_in_dim(finals[3], layer, micro_count, 0)
+    stored = lax.dynamic_update_index_in_dim(finals[3], finals[0], tick_count - 1, 0)
+    results = lax.dynamic_slice_in_dim(stored, layer, micro_count, 0)
     returned_home = lax.ppermute(results, "section", HOME)
     return jnp.where(here, results, returned_home)[None]
 

time: 863 us -> 832 us (0.964)
  waiting for transfers between devices: 545 us -> 520 us
    ppermute x10, waiting for transfers between devices: 434 us -> 409 us  [advance(): inbound = lax.ppermute(output_rows, 'section', RELAY)]
    dynamic_update_slice x11, local copies, waits for them, and re-layouts: 7.85 us -> 17.2 us  [the longest x10 15.7 us: advance(): lax.dynamic_update_index_in_dim(stored, output_rows, tick_index - 1, 0)]
    cond x26 -> x16, local copies, waits for them, and re-layouts: 13.7 us -> 4.62 us
    while x10 -> x0, local copies, waits for them, and re-layouts: 9.04 us -> none
  transfers between devices with their start and end apart: 22 -> 22, of which waited for: 19 -> 19; matrix products, arithmetic and copies ran while one was open for 7% -> 9% of each run, Pallas kernels for 0% -> 0%
where the time goes in v3:
time: 832 us; the launch traced here: 829 us
  waiting for transfers between devices  520 us (62%)
  blocking collectives  88.8 us (11%)
  starting transfers between devices  49.8 us (6%)
  matrix products  49.7 us (6%)
  local copies, waits for them, and re-layouts  46 us (6%)
  Pallas kernels  25.6 us (3%)
  other arithmetic  23.7 us (3%)
  between operations  16.4 us (2%)
  loops' own time  8.36 us (1%)
    ppermute x10, waiting for transfers between devices, advance(): inbound = lax.ppermute(output_rows, 'section', RELAY)  409 us
    all_to_all x4, blocking collectives, mixture(): lax.all_to_all(outgoing, 'expert', split_axis=0, concat_axis=0, tiled=True)  88.8 us
    ppermute x6, waiting for transfers between devices, relocated(): return jnp.where(here, value, lax.ppermute(value, 'section', MOVES))  74.1 us
    pallas_call x4, Pallas kernels, expert_rows(): pl.pallas_call(expert_kernel, out_shape=jax.ShapeDtypeStruct((count, mode...  25.6 us
    all_to_all x4, waiting for transfers between devices, mixture(): lax.all_to_all(produced, 'expert', split_axis=0, concat_axis=0, tiled=True)  23.9 us
    all_to_all x4, starting transfers between devices, mixture(): lax.all_to_all(produced, 'expert', split_axis=0, concat_axis=0, tiled=True)  20.1 us
  transfers between devices with their start and end apart: 22, of which 19 were waited for; matrix products, arithmetic and copies ran while one was open for 9% of the time, Pallas kernels for 0%

profile of v3, /device:TPU:13, one launch (start us, length us, event | category | flops | bytes accessed | tf_op | source)
XLA Modules:
  0.0 828.7 jit_solution(415258128018371566)
XLA Ops:
  20.6 4.2 collective-permute-start.1
  34.8 50.8 %collective-permute-done.6 = s32[4,32,12]{2,1,0:T(8,128)S(1)} collective-permute-done((s32[4,32,12]{2,1,0:T(8,128)S(1)}, s32[4,32,12]{2,1,0:T(8,128)S(1)}, u32[]{:S(2)}, u32[]{:S(2)}) %collective-permute-start.6) | collective-permute-done | bytes 6176 | tf_op jit(solution)/shard_map/ppermute | solution.py:142
  88.1 4.9 broadcast_select_fusion.2
  97.0 19.5 %collective-permute-done.5 = bf16[704,2048]{1,0:T(8,128)(2,1)} collective-permute-done((bf16[704,2048]{1,0:T(8,128)(2,1)}, bf16[704,2048]{1,0:T(8,128)(2,1)}, u32[]{:S(2)}, u32[]{:S(2)}) %collective-permute-start.5) | collective-permute-done | bytes 2883616 | tf_op jit(solution)/shard_map/ppermute | solution.py:142
  120.4 4.8 all-gather.2.cloned.1.call-done
  128.0 6.3 fusion.105
  137.5 669.9 %while.23 = (s32[]{:T(128)}, bf16[32,2048]{1,0:T(8,128)(2,1)}, bf16[128,128]{1,0:T(8,128)(2,1)}, bf16[128,128]{1,0:T(8,128)(2,1)}, bf16[11,32,2048]{2,1,0:T(8,12...) while((s32[]{:T(128)}, bf16[32,2048]{1,0:T(8,128)(2,1)}, ...), condition=%wide.region_15.16_spmd, body=%wide.region_9.15_spmd.sunk | while | flops 2610868480 | bytes 39272424 | solution.py:281
  140.9 10.7 %collective-permute-done = bf16[32,2048]{1,0:T(8,128)(2,1)S(1)} collective-permute-done((bf16[32,2048]{1,0:T(8,128)(2,1)}, bf16[32,2048]{1,0:T(8,128)(2,1)S(1)}, u32[]{:S(2)}, u32[]{:S(2)}) %collective-permute-start) | collective-permute-done | bytes 131104 | tf_op jit(solution)/shard_map/while/body/eval_jaxpr/ppermute | solution.py:261
  179.9 4.0 collective-permute-done
  196.1 362.7 %collective-permute-done = bf16[32,2048]{1,0:T(8,128)(2,1)S(1)} collective-permute-done((bf16[32,2048]{1,0:T(8,128)(2,1)}, bf16[32,2048]{1,0:T(8,128)(2,1)S(1)}, u32[]{:S(2)}, u32[]{:S(2)}) %collective-permute-start) | collective-permute-done | bytes 131104 | tf_op jit(solution)/shard_map/while/body/eval_jaxpr/ppermute | solution.py:261
  558.8 55.6 %conditional.6 = (bf16[128,128]{1,0:T(8,128)(2,1)}, bf16[128,128]{1,0:T(8,128)(2,1)}, bf16[32,2048]{1,0:T(8,128)(2,1)}) conditional(s32[]{:T(128)} %convert_element_type.219, (bf16[128,128]{1,0:T(8,128)(2,1)}, bf16[128,128]{1,0:T(8,128)(2,1)}) %tuple.104, (s32[]{:T(128)}, s32[]{:T(128)}, bf16[4,32,2048]{2,1,0:T(8,128)(2,1)}, ...), branch_computations={%region_10.10_spmd, %region_11.14_spmd} | conditional | flops 2610868480 | bytes 38485076 | solution.py:276
  561.6 22.2 %all_to_all.18 = bf16[32,8,2048]{2,1,0:T(8,128)(2,1)S(1)} all-to-all(bf16[32,8,2048]{2,1,0:T(8,128)(2,1)S(1)} %fusion.45), channel_id=1, replica_groups=mesh['section'=8,'expert'=32] {'expert'}, dimensions={0} | all-to-all | bytes 2097152 | tf_op jit(solution)/shard_map/while/body/eval_jaxpr/cond/branch_1_fun/all_to_all | solution.py:188
  583.9 6.4 experts.3
  590.3 5.0 all-to-all-start.3
  606.7 6.0 all-to-all-done.3
  621.7 55.5 %conditional.6 = (bf16[128,128]{1,0:T(8,128)(2,1)}, bf16[128,128]{1,0:T(8,128)(2,1)}, bf16[32,2048]{1,0:T(8,128)(2,1)}) conditional(s32[]{:T(128)} %convert_element_type.219, (bf16[128,128]{1,0:T(8,128)(2,1)}, bf16[128,128]{1,0:T(8,128)(2,1)}) %tuple.104, (s32[]{:T(128)}, s32[]{:T(128)}, bf16[4,32,2048]{2,1,0:T(8,128)(2,1)}, ...), branch_computations={%region_10.10_spmd, %region_11.14_spmd} | conditional | flops 2610868480 | bytes 38485076 | solution.py:276
  624.6 22.2 %all_to_all.18 = bf16[32,8,2048]{2,1,0:T(8,128)(2,1)S(1)} all-to-all(bf16[32,8,2048]{2,1,0:T(8,128)(2,1)S(1)} %fusion.45), channel_id=1, replica_groups=mesh['section'=8,'expert'=32] {'expert'}, dimensions={0} | all-to-all | bytes 2097152 | tf_op jit(solution)/shard_map/while/body/eval_jaxpr/cond/branch_1_fun/all_to_all | solution.py:188
  646.8 6.4 experts.3
  653.2 5.0 all-to-all-start.3
  669.6 6.0 all-to-all-done.3
  684.7 55.5 %conditional.6 = (bf16[128,128]{1,0:T(8,128)(2,1)}, bf16[128,128]{1,0:T(8,128)(2,1)}, bf16[32,2048]{1,0:T(8,128)(2,1)}) conditional(s32[]{:T(128)} %convert_element_type.219, (bf16[128,128]{1,0:T(8,128)(2,1)}, bf16[128,128]{1,0:T(8,128)(2,1)}) %tuple.104, (s32[]{:T(128)}, s32[]{:T(128)}, bf16[4,32,2048]{2,1,0:T(8,128)(2,1)}, ...), branch_computations={%region_10.10_spmd, %region_11.14_spmd} | conditional | flops 2610868480 | bytes 38485076 | solution.py:276
  687.5 22.2 %all_to_all.18 = bf16[32,8,2048]{2,1,0:T(8,128)(2,1)S(1)} all-to-all(bf16[32,8,2048]{2,1,0:T(8,128)(2,1)S(1)} %fusion.45), channel_id=1, replica_groups=mesh['section'=8,'expert'=32] {'expert'}, dimensions={0} | all-to-all | bytes 2097152 | tf_op jit(solution)/shard_map/while/body/eval_jaxpr/cond/branch_1_fun/all_to_all | solution.py:188
  709.7 6.4 experts.3
  716.1 5.0 all-to-all-start.3
  732.5 6.0 all-to-all-done.3
  743.6 8.2 collective-permute-done
  751.9 55.5 %conditional.6 = (bf16[128,128]{1,0:T(8,128)(2,1)}, bf16[128,128]{1,0:T(8,128)(2,1)}, bf16[32,2048]{1,0:T(8,128)(2,1)}) conditional(s32[]{:T(128)} %convert_element_type.219, (bf16[128,128]{1,0:T(8,128)(2,1)}, bf16[128,128]{1,0:T(8,128)(2,1)}) %tuple.104, (s32[]{:T(128)}, s32[]{:T(128)}, bf16[4,32,2048]{2,1,0:T(8,128)(2,1)}, ...), branch_computations={%region_10.10_spmd, %region_11.14_spmd} | conditional | flops 2610868480 | bytes 38485076 | solution.py:276
  754.7 22.2 %all_to_all.18 = bf16[32,8,2048]{2,1,0:T(8,128)(2,1)S(1)} all-to-all(bf16[32,8,2048]{2,1,0:T(8,128)(2,1)S(1)} %fusion.45), channel_id=1, replica_groups=mesh['section'=8,'expert'=32] {'expert'}, dimensions={0} | all-to-all | bytes 2097152 | tf_op jit(solution)/shard_map/while/body/eval_jaxpr/cond/branch_1_fun/all_to_all | solution.py:188
  776.9 6.4 experts.3
  783.3 5.0 all-to-all-start.3
  799.7 6.0 all-to-all-done.3
  811.9 8.0 collective-permute-done.7
  (165 shorter events, 167.3 us)
Async XLA Ops:
  6.5 21.2 %copy-start.9 = (s32[1,4,32,6]{2,1,3,0:T(4,128)S(1)}, s32[1,4,32,6]{2,1,3,0:T(4,128)}, u32[]{:S(2)}) copy-start(s32[1,4,32,6]{2,1,3,0:T(4,128)} %param.32) | copy-start | bytes 9220
  6.5 21.2 %copy-start.10 = (s32[1,4,32,6]{2,1,3,0:T(4,128)S(1)}, s32[1,4,32,6]{2,1,3,0:T(4,128)}, u32[]{:S(2)}) copy-start(s32[1,4,32,6]{2,1,3,0:T(4,128)} %param.31) | copy-start | bytes 9220
  6.5 118.7 %all-gather.2.cloned.1.call-start = ((), (), s32[]{:S(2)}) async-start(), calls=%async_computation.4 | async-start | bytes 9732096 | tf_op jit(solution)/shard_map/all_gather | solution.py:157
  7.4 80.6 %copy-start.7 = (f32[1,2048]{1,0:T(1,128)S(1)}, f32[1,2048]{1,0:T(1,128)}, u32[]{:S(2)}) copy-start(f32[1,2048]{1,0:T(1,128)} %param.23) | copy-start | bytes 24580
  7.5 80.5 %copy-start.8 = (f32[1,2048]{1,0:T(1,128)S(1)}, f32[1,2048]{1,0:T(1,128)}, u32[]{:S(2)}) copy-start(f32[1,2048]{1,0:T(1,128)} %param.22) | copy-start | bytes 24580
  8.4 7.8 collective-permute-start.2
  18.0 70.2 %collective-permute-start.3 = (bf16[704,2048]{1,0:T(8,128)(2,1)}, bf16[704,2048]{1,0:T(8,128)(2,1)}, u32[]{:S(2)}, u32[]{:S(2)}) collective-permute-start(bf16[704,2048]{1,0:T(8,128)(2,1)} %bitcast.176), channel_id=1, source_target_pairs={{32,192},{96,128},{128,224},{160,96},{192,32},{224,160},{33,193},{... | collective-permute-start | bytes 8650760 | tf_op jit(solution)/shard_map/ppermute | solution.py:142
  20.6 67.4 %collective-permute-start.1 = (f32[2,2048]{1,0:T(2,128)S(1)}, f32[2,2048]{1,0:T(2,128)S(1)}, u32[]{:S(2)}, u32[]{:S(2)}) collective-permute-start(f32[2,2048]{1,0:T(2,128)S(1)} %pad_maximum_fusion), channel_id=1, source_target_pairs={{32,192},{96,128},{128,224},{160,96},{192,32},{224,160},{33,193},{... | collective-permute-start | bytes 49160 | tf_op jit(solution)/shard_map/ppermute | solution.py:142
  24.8 68.2 %collective-permute-start.4 = (bf16[704,2048]{1,0:T(8,128)(2,1)}, bf16[704,2048]{1,0:T(8,128)(2,1)}, u32[]{:S(2)}, u32[]{:S(2)}) collective-permute-start(bf16[704,2048]{1,0:T(8,128)(2,1)} %bitcast.178), channel_id=1, source_target_pairs={{32,192},{96,128},{128,224},{160,96},{192,32},{224,160},{33,193},{... | collective-permute-start | bytes 8650760 | tf_op jit(solution)/shard_map/ppermute | solution.py:142
  27.8 57.8 %collective-permute-start.6 = (s32[4,32,12]{2,1,0:T(8,128)S(1)}, s32[4,32,12]{2,1,0:T(8,128)S(1)}, u32[]{:S(2)}, u32[]{:S(2)}) collective-permute-start(s32[4,32,12]{2,1,0:T(8,128)S(1)} %copy.41), channel_id=1, source_target_pairs={{32,192},{96,128},{128,224},{160,96},{192,32},{224,160},{33,193},{... | collective-permute-start | bytes 18440 | tf_op jit(solution)/shard_map/ppermute | solution.py:142
  32.9 83.6 %collective-permute-start.5 = (bf16[704,2048]{1,0:T(8,128)(2,1)}, bf16[704,2048]{1,0:T(8,128)(2,1)}, u32[]{:S(2)}, u32[]{:S(2)}) collective-permute-start(bf16[704,2048]{1,0:T(8,128)(2,1)} %bitcast.180), channel_id=1, source_target_pairs={{32,192},{96,128},{128,224},{160,96},{192,32},{224,160},{33,193},{... | collective-permute-start | bytes 8650760 | tf_op jit(solution)/shard_map/ppermute | solution.py:142
  88.1 4.9 copy-start.4
  93.0 23.5 %copy-start.5 = (bf16[1,1,704,2048]{3,2,1,0:T(8,128)(2,1)S(1)}, bf16[1,1,704,2048]{3,2,1,0:T(8,128)(2,1)}, u32[]{:S(2)}) copy-start(bf16[1,1,704,2048]{3,2,1,0:T(8,128)(2,1)} %param.30) | copy-start | bytes 8650756
  128.0 6.3 copy-start
  137.5 14.1 %collective-permute-start = (bf16[32,2048]{1,0:T(8,128)(2,1)}, bf16[32,2048]{1,0:T(8,128)(2,1)S(1)}, u32[]{:S(2)}, u32[]{:S(2)}) collective-permute-start(bf16[32,2048]{1,0:T(8,128)(2,1)} %get-tuple-element.872), channel_id=1, source_target_pairs={{0,192},{192,64},{64,128},{128,224},{224,96},{96,32},{32,160},{1,1... | collective-permute-start | bytes 393224 | tf_op jit(solution)/shard_map/while/body/eval_jaxpr/ppermute | solution.py:261
  152.2 7.4 collective-permute-start
  160.3 7.4 collective-permute-start
  168.4 7.4 collective-permute-start
  176.5 7.4 collective-permute-start
  184.6 7.4 collective-permute-start
  192.7 366.1 %collective-permute-start = (bf16[32,2048]{1,0:T(8,128)(2,1)}, bf16[32,2048]{1,0:T(8,128)(2,1)S(1)}, u32[]{:S(2)}, u32[]{:S(2)}) collective-permute-start(bf16[32,2048]{1,0:T(8,128)(2,1)} %get-tuple-element.872), channel_id=1, source_target_pairs={{0,192},{192,64},{64,128},{128,224},{224,96},{96,32},{32,160},{1,1... | collective-permute-start | bytes 393224 | tf_op jit(solution)/shard_map/while/body/eval_jaxpr/ppermute | solution.py:261
  590.3 22.4 %all-to-all-start.3 = ((bf16[32,8,2048]{2,1,0:T(8,128)(2,1)}), bf16[32,8,2048]{2,1,0:T(8,128)(2,1)S(1)}, u32[]{:S(2)}, u32[]{:S(2)}) async-start(bf16[32,8,2048]{2,1,0:T(8,128)(2,1)} %bitcast.25), calls=%async_computation.3 | async-start | bytes 2097152 | tf_op jit(solution)/shard_map/while/body/eval_jaxpr/cond/branch_1_fun/all_to_all | solution.py:191
  603.7 1.6 copy-start.2
  614.3 7.4 collective-permute-start
  653.2 22.4 %all-to-all-start.3 = ((bf16[32,8,2048]{2,1,0:T(8,128)(2,1)}), bf16[32,8,2048]{2,1,0:T(8,128)(2,1)S(1)}, u32[]{:S(2)}, u32[]{:S(2)}) async-start(bf16[32,8,2048]{2,1,0:T(8,128)(2,1)} %bitcast.25), calls=%async_computation.3 | async-start | bytes 2097152 | tf_op jit(solution)/shard_map/while/body/eval_jaxpr/cond/branch_1_fun/all_to_all | solution.py:191
  666.7 1.6 copy-start.2
  677.3 7.4 collective-permute-start
  716.1 22.4 %all-to-all-start.3 = ((bf16[32,8,2048]{2,1,0:T(8,128)(2,1)}), bf16[32,8,2048]{2,1,0:T(8,128)(2,1)S(1)}, u32[]{:S(2)}, u32[]{:S(2)}) async-start(bf16[32,8,2048]{2,1,0:T(8,128)(2,1)} %bitcast.25), calls=%async_computation.3 | async-start | bytes 2097152 | tf_op jit(solution)/shard_map/while/body/eval_jaxpr/cond/branch_1_fun/all_to_all | solution.py:191
  729.6 1.6 copy-start.2
  740.2 11.7 %collective-permute-start = (bf16[32,2048]{1,0:T(8,128)(2,1)}, bf16[32,2048]{1,0:T(8,128)(2,1)S(1)}, u32[]{:S(2)}, u32[]{:S(2)}) collective-permute-start(bf16[32,2048]{1,0:T(8,128)(2,1)} %get-tuple-element.872), channel_id=1, source_target_pairs={{0,192},{192,64},{64,128},{128,224},{224,96},{96,32},{32,160},{1,1... | collective-permute-start | bytes 393224 | tf_op jit(solution)/shard_map/while/body/eval_jaxpr/ppermute | solution.py:261
  783.3 22.4 %all-to-all-start.3 = ((bf16[32,8,2048]{2,1,0:T(8,128)(2,1)}), bf16[32,8,2048]{2,1,0:T(8,128)(2,1)S(1)}, u32[]{:S(2)}, u32[]{:S(2)}) async-start(bf16[32,8,2048]{2,1,0:T(8,128)(2,1)} %bitcast.25), calls=%async_computation.3 | async-start | bytes 2097152 | tf_op jit(solution)/shard_map/while/body/eval_jaxpr/cond/branch_1_fun/all_to_all | solution.py:191
  810.0 9.9 %collective-permute-start.7 = (bf16[4,32,2048]{2,1,0:T(8,128)(2,1)S(1)}, bf16[4,32,2048]{2,1,0:T(8,128)(2,1)S(1)}, u32[]{:S(2)}, u32[]{:S(2)}) collective-permute-start(bf16[4,32,2048]{2,1,0:T(8,128)(2,1)S(1)} %constant_dynamic-slice_fusion), channel_id=1, source_target_pairs={{192,32},{128,96},{224,128},{96,160},{32,192},{160,224},{193,33},{... | collective-permute-start | bytes 1572872 | tf_op jit(solution)/shard_map/ppermute | solution.py:284
  (5 other events, 4.2 us)
Sparse Core Ops, SparseCore 0:
  18.1 107.0 all-gather.1

commit v4 on v3

--- a/solution.py
+++ b/solution.py
@@ -13,8 +13,8 @@
 HOME = [(place, layer) for layer, place in MOVES]
 RELAY = [(POSITION[layer], POSITION[layer + 1]) for layer in range(7)]
 
-SPAN = 352
-FLIGHT = 3
+SPAN = 1024
+FLIGHT = 2
 
 
 def rms_normed(wide, gain_vector):
@@ -23,8 +23,20 @@
 
 
 def expert_kernel(
-    rows_ref, gate_hbm, up_hbm, down_hbm, out_ref, gate_buf, up_buf, down_buf, hidden_buf, sems
+    rows_ref,
+    gate_hbm,
+    up_hbm,
+    down_hbm,
+    attn_ref,
+    out_ref,
+    passed_ref,
+    gate_buf,
+    up_buf,
+    down_buf,
+    hidden_buf,
+    sems,
 ):
+    passed_ref[...] = attn_ref[...]
     hidden_width = down_buf.shape[0]
     spans = [
         pl.ds(first, min(SPAN, hidden_width - first)) for first in range(0, hidden_width, SPAN)
@@ -65,7 +77,7 @@
     ).astype(jnp.bfloat16)
 
 
-def expert_rows(rows, matrices):
+def expert_rows(rows, matrices, attn_rows):
     count, model_width = rows.shape
     hidden_width = matrices[2].shape[0]
     vmem = pl.BlockSpec(memory_space=pltpu.VMEM)
@@ -73,9 +85,12 @@
     copy_count = 3 * -(-hidden_width // SPAN)
     return pl.pallas_call(
         expert_kernel,
-        out_shape=jax.ShapeDtypeStruct((count, model_width), jnp.bfloat16),
-        in_specs=[vmem, anywhere, anywhere, anywhere],
-        out_specs=vmem,
+        out_shape=[
+            jax.ShapeDtypeStruct((count, model_width), jnp.bfloat16),
+            jax.ShapeDtypeStruct(attn_rows.shape, attn_rows.dtype),
+        ],
+        in_specs=[vmem, anywhere, anywhere, anywhere, vmem],
+        out_specs=[vmem, vmem],
         scratch_shapes=[
             pltpu.VMEM((hidden_width, model_width), jnp.bfloat16),
             pltpu.VMEM((hidden_width, model_width), jnp.bfloat16),
@@ -90,7 +105,61 @@
             transcendentals=count * hidden_width,
         ),
         name="experts",
-    )(rows, *matrices)
+    )(rows, *matrices, attn_rows)
+
+
+def send_kernel(
+    state_ref, inbound_ref, tokens_hbm, gain_ref, table_ref, out_ref, rows_ref, attn_ref, sem
+):
+    leading, block = state_ref[0], state_ref[1]
+
+    @pl.when(leading != 0)
+    def _():
+        copy = pltpu.make_async_copy(tokens_hbm.at[block], rows_ref, sem)
+        copy.start()
+        copy.wait()
+
+    @pl.when(leading == 0)
+    def _():
+        rows_ref[...] = inbound_ref[...]
+
+    wide = rows_ref[...].astype(jnp.float32)
+    scaled = wide * lax.rsqrt(jnp.mean(wide * wide, axis=-1, keepdims=True) + epsilon)
+    attn_ref[...] = (scaled * gain_ref[0:1, :]).astype(jnp.bfloat16)
+    normed = (scaled * gain_ref[1:2, :]).astype(jnp.bfloat16)
+    out_ref[...] = jnp.dot(
+        table_ref[block], normed, preferred_element_type=jnp.float32
+    ).astype(jnp.bfloat16)
+
+
+def rows_to_send(state, inbound, tokens, gain, tables):
+    vmem = pl.BlockSpec(memory_space=pltpu.VMEM)
+    slot_count = tables.shape[1]
+    tok_rows, model_width = inbound.shape
+    return pl.pallas_call(
+        send_kernel,
+        out_shape=[
+            jax.ShapeDtypeStruct((slot_count, model_width), jnp.bfloat16),
+            jax.ShapeDtypeStruct((tok_rows, model_width), jnp.bfloat16),
+            jax.ShapeDtypeStruct((tok_rows, model_width), jnp.bfloat16),
+        ],
+        in_specs=[
+            pl.BlockSpec(memory_space=pltpu.SMEM),
+            vmem,
+            pl.BlockSpec(memory_space=pl.ANY),
+            vmem,
+            vmem,
+        ],
+        out_specs=[vmem] * 3,
+        scratch_shapes=[pltpu.SemaphoreType.DMA],
+        compiler_params=pltpu.CompilerParams(vmem_limit_bytes=12 * 2**20),
+        cost_estimate=pl.CostEstimate(
+            flops=2 * slot_count * tok_rows * model_width,
+            bytes_accessed=2 * (slot_count + 3 * tok_rows) * model_width,
+            transcendentals=tok_rows,
+        ),
+        name="send",
+    )(state, inbound, tokens, gain, tables)
 
 
 def route_tables(picks, codes, expert_count, capacity):
@@ -157,11 +226,13 @@
     full = lax.all_gather(relocated(packed), "expert", axis=0, tiled=True)
     tables = relocated(jnp.concatenate([routes[0], weights_code[0]], axis=-1))
     gains = relocated(jnp.concatenate([attn_norm, moe_norm], axis=0))
-    attn_gain, moe_gain = gains[0], gains[1]
+    attn_gain = gains[0]
     scatter_tables, combine_tables = route_tables(
         tables[:, :, :pick_count], tables[:, :, pick_count:], expert_count, capacity
     )
-    scatter_tables, combine_tables = lax.optimization_barrier((scatter_tables, combine_tables))
+    scatter_tables, combine_tables = lax.optimization_barrier(
+        (jnp.swapaxes(scatter_tables, 1, 2), combine_tables)
+    )
     own = (gate_proj[0, 0].T, up_proj[0, 0].T, down_proj[0, 0])
     here_matrices = tuple(relocated(value) for value in own)
 
@@ -178,23 +249,23 @@
         )
         return (full[:, :score_width], outer)
 
-    def mixture(layer_input, block, matrices):
-        wide = layer_input.astype(jnp.float32)
-        normed = rms_normed(wide, moe_gain)
-        scatter_table = lax.dynamic_index_in_dim(scatter_tables, block, 0, keepdims=False)
+    def mixture(inbound, leads, block, matrices):
         combine_table = lax.dynamic_index_in_dim(combine_tables, block, 0, keepdims=False)
-        outgoing = jnp.einsum("te,td->ed", scatter_table, normed, preferred_element_type=jnp.float32)
-        outgoing = outgoing.astype(jnp.bfloat16).reshape(expert_count, capacity, model_width)
+        state = jnp.stack([leads.astype(jnp.int32), block])
+        outgoing, layer_input, attn_rows = rows_to_send(
+            state, inbound, tokens, gains, scatter_tables
+        )
+        outgoing = outgoing.reshape(expert_count, capacity, model_width)
         arrived = lax.all_to_all(outgoing, "expert", split_axis=0, concat_axis=0, tiled=True)
-        produced = expert_rows(arrived.reshape(-1, model_width), matrices)
+        produced, attn_rows = expert_rows(arrived.reshape(-1, model_width), matrices, attn_rows)
         produced = produced.reshape(arrived.shape)
         returned = lax.all_to_all(produced, "expert", split_axis=0, concat_axis=0, tiled=True)
-        return jnp.dot(
+        mixed = jnp.dot(
             combine_table, returned.reshape(-1, model_width), preferred_element_type=jnp.float32
         )
-
-    def attend(layer_input, block, old_keys, old_values, inner, outer):
-        normed = rms_normed(layer_input.astype(jnp.float32), attn_gain)
+        return (mixed, layer_input, attn_rows)
+
+    def attend(normed, block, old_keys, old_values, inner, outer):
         projected = jnp.dot(normed, inner, preferred_element_type=jnp.float32)
         projected = projected.astype(jnp.bfloat16)
         query_rows = projected[:, : head_count * head_size]
@@ -233,7 +304,7 @@
     first_rows = tokens[0]
     mixed = lax.cond(
         leading,
-        lambda rows: mixture(rows, first_block, own),
+        lambda rows: mixture(rows, jnp.bool_(False), first_block, own)[0],
         lambda rows: jnp.zeros((tok_rows, model_width), jnp.float32),
         first_rows,
     )
@@ -242,7 +313,8 @@
 
     def first_attend(arrays):
         rows, mixed, keys, values = arrays
-        attended, keys, values = attend(rows, first_block, keys, values, inner, outer)
+        normed = rms_normed(rows.astype(jnp.float32), attn_gain)
+        attended, keys, values = attend(normed, first_block, keys, values, inner, outer)
         return (rows.astype(jnp.float32) + attended + mixed, keys, values)
 
     nothing = jnp.zeros((tok_rows, model_width), jnp.float32)
@@ -266,10 +338,8 @@
 
         def work(arrays):
             inbound, keys, values = arrays
-            held = lax.dynamic_index_in_dim(tokens, block, 0, keepdims=False)
-            layer_input = jnp.where(layer == 0, held, inbound)
-            mixed = mixture(layer_input, block, here_matrices)
-            attended, keys, values = attend(layer_input, block, keys, values, inner, outer)
+            mixed, layer_input, attn_rows = mixture(inbound, layer == 0, block, here_matrices)
+            attended, keys, values = attend(attn_rows, block, keys, values, inner, outer)
             output_rows = layer_input.astype(jnp.float32) + attended + mixed
             return (output_rows, keys, values)
 

time: 832 us -> 824 us (level)
  matrix products: 49.7 us -> 41.1 us
    pallas_call x4 -> x8, Pallas kernels: 25.6 us -> 31.7 us  [the longest x4 25.6 us: expert_rows(): pl.pallas_call(expert_kernel, out_shape=[jax.ShapeDtypeStruct((count, mod...]
where the time goes in v4:
time: 824 us; the launch traced here: 821 us
  waiting for transfers between devices  518 us (63%)
  blocking collectives  88.7 us (11%)
  starting transfers between devices  49.8 us (6%)
  local copies, waits for them, and re-layouts  46 us (6%)
  matrix products  41.1 us (5%)
  Pallas kernels  31.7 us (4%)
  other arithmetic  20.6 us (2%)
  between operations  16.4 us (2%)
  loops' own time  8.39 us (1%)
    ppermute x10, waiting for transfers between devices, advance(): inbound = lax.ppermute(output_rows, 'section', RELAY)  405 us
    all_to_all x4, blocking collectives, mixture(): lax.all_to_all(outgoing, 'expert', split_axis=0, concat_axis=0, tiled=True)  88.7 us
    ppermute x6, waiting for transfers between devices, relocated(): return jnp.where(here, value, lax.ppermute(value, 'section', MOVES))  73.1 us
    all_to_all x4, waiting for transfers between devices, mixture(): lax.all_to_all(produced, 'expert', split_axis=0, concat_axis=0, tiled=True)  27.7 us
    pallas_call x4, Pallas kernels, expert_rows(): pl.pallas_call(expert_kernel, out_shape=[jax.ShapeDtypeStruct((count, mod...  25.6 us
    all_to_all x4, starting transfers between devices, mixture(): lax.all_to_all(produced, 'expert', split_axis=0, concat_axis=0, tiled=True)  20.1 us
  transfers between devices with their start and end apart: 22, of which 19 were waited for; matrix products, arithmetic and copies ran while one was open for 9% of the time, Pallas kernels for 0%

profile of v4, /device:TPU:13, one launch (start us, length us, event | category | flops | bytes accessed | tf_op | source)
XLA Modules:
  0.0 820.8 jit_solution(3804463216042394987)
XLA Ops:
  20.6 4.2 collective-permute-start.1
  34.8 50.8 %collective-permute-done.6 = s32[4,32,12]{2,1,0:T(8,128)S(1)} collective-permute-done((s32[4,32,12]{2,1,0:T(8,128)S(1)}, s32[4,32,12]{2,1,0:T(8,128)S(1)}, u32[]{:S(2)}, u32[]{:S(2)}) %collective-permute-start.6) | collective-permute-done | bytes 6176 | tf_op jit(solution)/shard_map/ppermute | solution.py:211
  89.1 4.8 broadcast_select_fusion.2
  93.9 4.0 broadcast_select_fusion.1
  97.9 18.6 %collective-permute-done.5 = bf16[704,2048]{1,0:T(8,128)(2,1)} collective-permute-done((bf16[704,2048]{1,0:T(8,128)(2,1)}, bf16[704,2048]{1,0:T(8,128)(2,1)}, u32[]{:S(2)}, u32[]{:S(2)}) %collective-permute-start.5) | collective-permute-done | bytes 2883616 | tf_op jit(solution)/shard_map/ppermute | solution.py:211
  127.1 6.3 fusion.81
  136.5 662.9 %while.23 = (s32[]{:T(128)}, bf16[32,2048]{1,0:T(8,128)(2,1)}, bf16[128,128]{1,0:T(8,128)(2,1)}, bf16[128,128]{1,0:T(8,128)(2,1)}, bf16[11,32,2048]{2,1,0:T(8,12...) while((s32[]{:T(128)}, bf16[32,2048]{1,0:T(8,128)(2,1)}, ...), condition=%wide.region_13.14_spmd, body=%wide.region_8.13_spmd.sunk | while | flops 2609557760 | bytes 39108448 | solution.py:351
  139.9 10.7 %collective-permute-done = bf16[32,2048]{1,0:T(8,128)(2,1)S(1)} collective-permute-done((bf16[32,2048]{1,0:T(8,128)(2,1)}, bf16[32,2048]{1,0:T(8,128)(2,1)S(1)}, u32[]{:S(2)}, u32[]{:S(2)}) %collective-permute-start) | collective-permute-done | bytes 131104 | tf_op jit(solution)/shard_map/while/body/eval_jaxpr/ppermute | solution.py:333
  178.9 4.0 collective-permute-done
  195.1 358.4 %collective-permute-done = bf16[32,2048]{1,0:T(8,128)(2,1)S(1)} collective-permute-done((bf16[32,2048]{1,0:T(8,128)(2,1)}, bf16[32,2048]{1,0:T(8,128)(2,1)S(1)}, u32[]{:S(2)}, u32[]{:S(2)}) %collective-permute-start) | collective-permute-done | bytes 131104 | tf_op jit(solution)/shard_map/while/body/eval_jaxpr/ppermute | solution.py:333
  553.5 54.8 %conditional.6 = (bf16[128,128]{1,0:T(8,128)(2,1)}, bf16[128,128]{1,0:T(8,128)(2,1)}, bf16[32,2048]{1,0:T(8,128)(2,1)}) conditional(s32[]{:T(128)} %convert_element_type.167, (bf16[128,128]{1,0:T(8,128)(2,1)}, bf16[128,128]{1,0:T(8,128)(2,1)}) %tuple.101, (s32[]{:T(128)}, s32[]{:T(128)}, bf16[32,2048]{1,0:T(8,128)(2,1)S(1)}, ...), branch_computations={%region_9.9_spmd, %region_10.12_spmd} | conditional | flops 2609557760 | bytes 38321116 | solution.py:346
  555.6 22.2 %all_to_all.18 = bf16[32,8,2048]{2,1,0:T(8,128)(2,1)S(1)} all-to-all(bf16[32,8,2048]{2,1,0:T(8,128)(2,1)S(1)} %bitcast.157), channel_id=1, replica_groups=mesh['section'=8,'expert'=32] {'expert'}, dimensions={0} | all-to-all | bytes 2097152 | tf_op jit(solution)/shard_map/while/body/eval_jaxpr/cond/branch_1_fun/all_to_all | solution.py:259
  577.8 6.4 experts.3
  584.2 5.0 all-to-all-start.3
  599.7 6.9 all-to-all-done.3
  615.7 54.8 %conditional.6 = (bf16[128,128]{1,0:T(8,128)(2,1)}, bf16[128,128]{1,0:T(8,128)(2,1)}, bf16[32,2048]{1,0:T(8,128)(2,1)}) conditional(s32[]{:T(128)} %convert_element_type.167, (bf16[128,128]{1,0:T(8,128)(2,1)}, bf16[128,128]{1,0:T(8,128)(2,1)}) %tuple.101, (s32[]{:T(128)}, s32[]{:T(128)}, bf16[32,2048]{1,0:T(8,128)(2,1)S(1)}, ...), branch_computations={%region_9.9_spmd, %region_10.12_spmd} | conditional | flops 2609557760 | bytes 38321116 | solution.py:346
  617.9 22.2 %all_to_all.18 = bf16[32,8,2048]{2,1,0:T(8,128)(2,1)S(1)} all-to-all(bf16[32,8,2048]{2,1,0:T(8,128)(2,1)S(1)} %bitcast.157), channel_id=1, replica_groups=mesh['section'=8,'expert'=32] {'expert'}, dimensions={0} | all-to-all | bytes 2097152 | tf_op jit(solution)/shard_map/while/body/eval_jaxpr/cond/branch_1_fun/all_to_all | solution.py:259
  640.1 6.4 experts.3
  646.5 5.0 all-to-all-start.3
  661.9 6.9 all-to-all-done.3
  678.0 54.8 %conditional.6 = (bf16[128,128]{1,0:T(8,128)(2,1)}, bf16[128,128]{1,0:T(8,128)(2,1)}, bf16[32,2048]{1,0:T(8,128)(2,1)}) conditional(s32[]{:T(128)} %convert_element_type.167, (bf16[128,128]{1,0:T(8,128)(2,1)}, bf16[128,128]{1,0:T(8,128)(2,1)}) %tuple.101, (s32[]{:T(128)}, s32[]{:T(128)}, bf16[32,2048]{1,0:T(8,128)(2,1)S(1)}, ...), branch_computations={%region_9.9_spmd, %region_10.12_spmd} | conditional | flops 2609557760 | bytes 38321116 | solution.py:346
  680.1 22.2 %all_to_all.18 = bf16[32,8,2048]{2,1,0:T(8,128)(2,1)S(1)} all-to-all(bf16[32,8,2048]{2,1,0:T(8,128)(2,1)S(1)} %bitcast.157), channel_id=1, replica_groups=mesh['section'=8,'expert'=32] {'expert'}, dimensions={0} | all-to-all | bytes 2097152 | tf_op jit(solution)/shard_map/while/body/eval_jaxpr/cond/branch_1_fun/all_to_all | solution.py:259
  702.3 6.4 experts.3
  708.7 5.0 all-to-all-start.3
  724.2 6.9 all-to-all-done.3
  736.2 8.4 %collective-permute-done = bf16[32,2048]{1,0:T(8,128)(2,1)S(1)} collective-permute-done((bf16[32,2048]{1,0:T(8,128)(2,1)}, bf16[32,2048]{1,0:T(8,128)(2,1)S(1)}, u32[]{:S(2)}, u32[]{:S(2)}) %collective-permute-start) | collective-permute-done | bytes 131104 | tf_op jit(solution)/shard_map/while/body/eval_jaxpr/ppermute | solution.py:333
  744.6 54.8 %conditional.6 = (bf16[128,128]{1,0:T(8,128)(2,1)}, bf16[128,128]{1,0:T(8,128)(2,1)}, bf16[32,2048]{1,0:T(8,128)(2,1)}) conditional(s32[]{:T(128)} %convert_element_type.167, (bf16[128,128]{1,0:T(8,128)(2,1)}, bf16[128,128]{1,0:T(8,128)(2,1)}) %tuple.101, (s32[]{:T(128)}, s32[]{:T(128)}, bf16[32,2048]{1,0:T(8,128)(2,1)S(1)}, ...), branch_computations={%region_9.9_spmd, %region_10.12_spmd} | conditional | flops 2609557760 | bytes 38321116 | solution.py:346
  746.8 22.2 %all_to_all.18 = bf16[32,8,2048]{2,1,0:T(8,128)(2,1)S(1)} all-to-all(bf16[32,8,2048]{2,1,0:T(8,128)(2,1)S(1)} %bitcast.157), channel_id=1, replica_groups=mesh['section'=8,'expert'=32] {'expert'}, dimensions={0} | all-to-all | bytes 2097152 | tf_op jit(solution)/shard_map/while/body/eval_jaxpr/cond/branch_1_fun/all_to_all | solution.py:259
  769.0 6.4 experts.3
  775.4 5.0 all-to-all-start.3
  790.8 6.9 all-to-all-done.3
  804.0 8.0 collective-permute-done.7
  (161 shorter events, 161.7 us)
Async XLA Ops:
  6.5 21.2 %copy-start.9 = (s32[1,4,32,6]{2,1,3,0:T(4,128)S(1)}, s32[1,4,32,6]{2,1,3,0:T(4,128)}, u32[]{:S(2)}) copy-start(s32[1,4,32,6]{2,1,3,0:T(4,128)} %param.32) | copy-start | bytes 9220
  6.5 21.2 %copy-start.10 = (s32[1,4,32,6]{2,1,3,0:T(4,128)S(1)}, s32[1,4,32,6]{2,1,3,0:T(4,128)}, u32[]{:S(2)}) copy-start(s32[1,4,32,6]{2,1,3,0:T(4,128)} %param.31) | copy-start | bytes 9220
  6.5 117.7 %all-gather.2.cloned.1.call-start = ((), (), s32[]{:S(2)}) async-start(), calls=%async_computation.4 | async-start | bytes 9732096 | tf_op jit(solution)/shard_map/all_gather | solution.py:226
  7.4 81.5 %copy-start.7 = (f32[1,2048]{1,0:T(1,128)S(1)}, f32[1,2048]{1,0:T(1,128)}, u32[]{:S(2)}) copy-start(f32[1,2048]{1,0:T(1,128)} %param.23) | copy-start | bytes 24580
  7.5 81.5 %copy-start.8 = (f32[1,2048]{1,0:T(1,128)S(1)}, f32[1,2048]{1,0:T(1,128)}, u32[]{:S(2)}) copy-start(f32[1,2048]{1,0:T(1,128)} %param.22) | copy-start | bytes 24580
  8.4 7.8 collective-permute-start.2
  18.0 71.1 %collective-permute-start.3 = (bf16[704,2048]{1,0:T(8,128)(2,1)}, bf16[704,2048]{1,0:T(8,128)(2,1)}, u32[]{:S(2)}, u32[]{:S(2)}) collective-permute-start(bf16[704,2048]{1,0:T(8,128)(2,1)} %bitcast.165), channel_id=1, source_target_pairs={{32,192},{96,128},{128,224},{160,96},{192,32},{224,160},{33,193},{... | collective-permute-start | bytes 8650760 | tf_op jit(solution)/shard_map/ppermute | solution.py:211
  20.6 68.4 %collective-permute-start.1 = (f32[2,2048]{1,0:T(2,128)S(1)}, f32[2,2048]{1,0:T(2,128)S(1)}, u32[]{:S(2)}, u32[]{:S(2)}) collective-permute-start(f32[2,2048]{1,0:T(2,128)S(1)} %pad_maximum_fusion), channel_id=1, source_target_pairs={{32,192},{96,128},{128,224},{160,96},{192,32},{224,160},{33,193},{... | collective-permute-start | bytes 49160 | tf_op jit(solution)/shard_map/ppermute | solution.py:211
  24.8 69.1 %collective-permute-start.4 = (bf16[704,2048]{1,0:T(8,128)(2,1)}, bf16[704,2048]{1,0:T(8,128)(2,1)}, u32[]{:S(2)}, u32[]{:S(2)}) collective-permute-start(bf16[704,2048]{1,0:T(8,128)(2,1)} %bitcast.167), channel_id=1, source_target_pairs={{32,192},{96,128},{128,224},{160,96},{192,32},{224,160},{33,193},{... | collective-permute-start | bytes 8650760 | tf_op jit(solution)/shard_map/ppermute | solution.py:211
  27.8 57.8 %collective-permute-start.6 = (s32[4,32,12]{2,1,0:T(8,128)S(1)}, s32[4,32,12]{2,1,0:T(8,128)S(1)}, u32[]{:S(2)}, u32[]{:S(2)}) collective-permute-start(s32[4,32,12]{2,1,0:T(8,128)S(1)} %copy.41), channel_id=1, source_target_pairs={{32,192},{96,128},{128,224},{160,96},{192,32},{224,160},{33,193},{... | collective-permute-start | bytes 18440 | tf_op jit(solution)/shard_map/ppermute | solution.py:211
  32.9 83.6 %collective-permute-start.5 = (bf16[704,2048]{1,0:T(8,128)(2,1)}, bf16[704,2048]{1,0:T(8,128)(2,1)}, u32[]{:S(2)}, u32[]{:S(2)}) collective-permute-start(bf16[704,2048]{1,0:T(8,128)(2,1)} %bitcast.169), channel_id=1, source_target_pairs={{32,192},{96,128},{128,224},{160,96},{192,32},{224,160},{33,193},{... | collective-permute-start | bytes 8650760 | tf_op jit(solution)/shard_map/ppermute | solution.py:211
  89.1 4.8 copy-start.4
  93.9 22.6 %copy-start.5 = (bf16[1,1,704,2048]{3,2,1,0:T(8,128)(2,1)S(1)}, bf16[1,1,704,2048]{3,2,1,0:T(8,128)(2,1)}, u32[]{:S(2)}) copy-start(bf16[1,1,704,2048]{3,2,1,0:T(8,128)(2,1)} %param.30) | copy-start | bytes 8650756
  127.1 6.3 copy-start
  136.5 14.1 %collective-permute-start = (bf16[32,2048]{1,0:T(8,128)(2,1)}, bf16[32,2048]{1,0:T(8,128)(2,1)S(1)}, u32[]{:S(2)}, u32[]{:S(2)}) collective-permute-start(bf16[32,2048]{1,0:T(8,128)(2,1)} %get-tuple-element.837), channel_id=1, source_target_pairs={{0,192},{192,64},{64,128},{128,224},{224,96},{96,32},{32,160},{1,1... | collective-permute-start | bytes 393224 | tf_op jit(solution)/shard_map/while/body/eval_jaxpr/ppermute | solution.py:333
  151.3 7.4 collective-permute-start
  159.3 7.4 collective-permute-start
  167.4 7.4 collective-permute-start
  175.5 7.4 collective-permute-start
  183.6 7.4 collective-permute-start
  191.7 361.8 %collective-permute-start = (bf16[32,2048]{1,0:T(8,128)(2,1)}, bf16[32,2048]{1,0:T(8,128)(2,1)S(1)}, u32[]{:S(2)}, u32[]{:S(2)}) collective-permute-start(bf16[32,2048]{1,0:T(8,128)(2,1)} %get-tuple-element.837), channel_id=1, source_target_pairs={{0,192},{192,64},{64,128},{128,224},{224,96},{96,32},{32,160},{1,1... | collective-permute-start | bytes 393224 | tf_op jit(solution)/shard_map/while/body/eval_jaxpr/ppermute | solution.py:333
  584.2 22.4 %all-to-all-start.3 = ((bf16[32,8,2048]{2,1,0:T(8,128)(2,1)}), bf16[32,8,2048]{2,1,0:T(8,128)(2,1)S(1)}, u32[]{:S(2)}, u32[]{:S(2)}) async-start(bf16[32,8,2048]{2,1,0:T(8,128)(2,1)} %bitcast.20), calls=%async_computation.3 | async-start | bytes 2097152 | tf_op jit(solution)/shard_map/while/body/eval_jaxpr/cond/branch_1_fun/all_to_all | solution.py:262
  596.8 1.6 copy-start.2
  608.3 7.4 collective-permute-start
  646.5 22.4 %all-to-all-start.3 = ((bf16[32,8,2048]{2,1,0:T(8,128)(2,1)}), bf16[32,8,2048]{2,1,0:T(8,128)(2,1)S(1)}, u32[]{:S(2)}, u32[]{:S(2)}) async-start(bf16[32,8,2048]{2,1,0:T(8,128)(2,1)} %bitcast.20), calls=%async_computation.3 | async-start | bytes 2097152 | tf_op jit(solution)/shard_map/while/body/eval_jaxpr/cond/branch_1_fun/all_to_all | solution.py:262
  659.0 1.6 copy-start.2
  670.5 7.4 collective-permute-start
  708.7 22.4 %all-to-all-start.3 = ((bf16[32,8,2048]{2,1,0:T(8,128)(2,1)}), bf16[32,8,2048]{2,1,0:T(8,128)(2,1)S(1)}, u32[]{:S(2)}, u32[]{:S(2)}) async-start(bf16[32,8,2048]{2,1,0:T(8,128)(2,1)} %bitcast.20), calls=%async_computation.3 | async-start | bytes 2097152 | tf_op jit(solution)/shard_map/while/body/eval_jaxpr/cond/branch_1_fun/all_to_all | solution.py:262
  721.3 1.6 copy-start.2
  732.8 11.8 %collective-permute-start = (bf16[32,2048]{1,0:T(8,128)(2,1)}, bf16[32,2048]{1,0:T(8,128)(2,1)S(1)}, u32[]{:S(2)}, u32[]{:S(2)}) collective-permute-start(bf16[32,2048]{1,0:T(8,128)(2,1)} %get-tuple-element.837), channel_id=1, source_target_pairs={{0,192},{192,64},{64,128},{128,224},{224,96},{96,32},{32,160},{1,1... | collective-permute-start | bytes 393224 | tf_op jit(solution)/shard_map/while/body/eval_jaxpr/ppermute | solution.py:333
  775.4 22.4 %all-to-all-start.3 = ((bf16[32,8,2048]{2,1,0:T(8,128)(2,1)}), bf16[32,8,2048]{2,1,0:T(8,128)(2,1)S(1)}, u32[]{:S(2)}, u32[]{:S(2)}) async-start(bf16[32,8,2048]{2,1,0:T(8,128)(2,1)} %bitcast.20), calls=%async_computation.3 | async-start | bytes 2097152 | tf_op jit(solution)/shard_map/while/body/eval_jaxpr/cond/branch_1_fun/all_to_all | solution.py:262
  802.1 9.9 %collective-permute-start.7 = (bf16[4,32,2048]{2,1,0:T(8,128)(2,1)S(1)}, bf16[4,32,2048]{2,1,0:T(8,128)(2,1)S(1)}, u32[]{:S(2)}, u32[]{:S(2)}) collective-permute-start(bf16[4,32,2048]{2,1,0:T(8,128)(2,1)S(1)} %constant_dynamic-slice_fusion), channel_id=1, source_target_pairs={{192,32},{128,96},{224,128},{96,160},{32,192},{160,224},{193,33},{... | collective-permute-start | bytes 1572872 | tf_op jit(solution)/shard_map/ppermute | solution.py:354
  (5 other events, 4.2 us)
Sparse Core Ops, SparseCore 0:
  18.1 106.1 all-gather.1

commit v5 on v4

--- a/solution.py
+++ b/solution.py
@@ -109,17 +109,26 @@
 
 
 def send_kernel(
-    state_ref, inbound_ref, tokens_hbm, gain_ref, table_ref, out_ref, rows_ref, attn_ref, sem
+    layer_ref,
+    block_ref,
+    inbound_ref,
+    tokens_hbm,
+    gain_ref,
+    table_ref,
+    out_ref,
+    rows_ref,
+    attn_ref,
+    sem,
 ):
-    leading, block = state_ref[0], state_ref[1]
-
-    @pl.when(leading != 0)
+    layer, block = layer_ref[0], block_ref[0]
+
+    @pl.when(layer == 0)
     def _():
         copy = pltpu.make_async_copy(tokens_hbm.at[block], rows_ref, sem)
         copy.start()
         copy.wait()
 
-    @pl.when(leading == 0)
+    @pl.when(layer != 0)
     def _():
         rows_ref[...] = inbound_ref[...]
 
@@ -132,7 +141,7 @@
     ).astype(jnp.bfloat16)
 
 
-def rows_to_send(state, inbound, tokens, gain, tables):
+def rows_to_send(layer, block, inbound, tokens, gain, tables):
     vmem = pl.BlockSpec(memory_space=pltpu.VMEM)
     slot_count = tables.shape[1]
     tok_rows, model_width = inbound.shape
@@ -145,6 +154,7 @@
         ],
         in_specs=[
             pl.BlockSpec(memory_space=pltpu.SMEM),
+            pl.BlockSpec(memory_space=pltpu.SMEM),
             vmem,
             pl.BlockSpec(memory_space=pl.ANY),
             vmem,
@@ -159,7 +169,7 @@
             transcendentals=tok_rows,
         ),
         name="send",
-    )(state, inbound, tokens, gain, tables)
+    )(layer.reshape(1), block.reshape(1), inbound, tokens, gain, tables)
 
 
 def route_tables(picks, codes, expert_count, capacity):
@@ -249,11 +259,10 @@
         )
         return (full[:, :score_width], outer)
 
-    def mixture(inbound, leads, block, matrices):
+    def mixture(inbound, block, matrices):
         combine_table = lax.dynamic_index_in_dim(combine_tables, block, 0, keepdims=False)
-        state = jnp.stack([leads.astype(jnp.int32), block])
         outgoing, layer_input, attn_rows = rows_to_send(
-            state, inbound, tokens, gains, scatter_tables
+            layer, block, inbound, tokens, gains, scatter_tables
         )
         outgoing = outgoing.reshape(expert_count, capacity, model_width)
         arrived = lax.all_to_all(outgoing, "expert", split_axis=0, concat_axis=0, tiled=True)
@@ -304,7 +313,7 @@
     first_rows = tokens[0]
     mixed = lax.cond(
         leading,
-        lambda rows: mixture(rows, jnp.bool_(False), first_block, own)[0],
+        lambda rows: mixture(rows, first_block, own)[0],
         lambda rows: jnp.zeros((tok_rows, model_width), jnp.float32),
         first_rows,
     )
@@ -328,27 +337,30 @@
     stored = jnp.zeros((tick_count, tok_rows, model_width), jnp.bfloat16)
     output_rows = total.astype(jnp.bfloat16)
 
-    def advance(tick_index, state_carry):
+    def advance(tick_index, inbound, keys, values):
+        block_index = tick_index - layer
+        active = (block_index >= 0) & (block_index < micro_count)
+        block = jnp.clip(block_index, 0, micro_count - 1)
+
+        def work(arrays):
+            inbound, keys, values = arrays
+            mixed, layer_input, attn_rows = mixture(inbound, block, here_matrices)
+            attended, keys, values = attend(attn_rows, block, keys, values, inner, outer)
+            output_rows = layer_input.astype(jnp.float32) + attended + mixed
+            return (output_rows, keys, values)
+
+        total, keys, values = lax.cond(
+            active, work, lambda arrays: (nothing, *arrays[1:]), (inbound, keys, values)
+        )
+        return (total.astype(jnp.bfloat16), keys, values)
+
+    def tick(tick_index, state_carry):
         output_rows, keys, values, stored = state_carry
         inbound = lax.ppermute(output_rows, "section", RELAY)
         stored = lax.dynamic_update_index_in_dim(stored, output_rows, tick_index - 1, 0)
-        block_index = tick_index - layer
-        active = (block_index >= 0) & (block_index < micro_count)
-        block = jnp.clip(block_index, 0, micro_count - 1)
-
-        def work(arrays):
-            inbound, keys, values = arrays
-            mixed, layer_input, attn_rows = mixture(inbound, layer == 0, block, here_matrices)
-            attended, keys, values = attend(attn_rows, block, keys, values, inner, outer)
-            output_rows = layer_input.astype(jnp.float32) + attended + mixed
-            return (output_rows, keys, values)
-
-        total, keys, values = lax.cond(
-            active, work, lambda arrays: (nothing, *arrays[1:]), (inbound, keys, values)
-        )
-        return (total.astype(jnp.bfloat16), keys, values, stored)
-
-    finals = lax.fori_loop(1, tick_count, advance, (output_rows, keys, values, stored))
+        return (*advance(tick_index, inbound, keys, values), stored)
+
+    finals = lax.fori_loop(1, tick_count, tick, (output_rows, keys, values, stored))
     stored = lax.dynamic_update_index_in_dim(finals[3], finals[0], tick_count - 1, 0)
     results = lax.dynamic_slice_in_dim(stored, layer, micro_count, 0)
     returned_home = lax.ppermute(results, "section", HOME)

time: 824 us -> 824 us (level)
  no operation moved by 1% of the time
where the time goes in v5:
time: 824 us; the launch traced here: 821 us
  waiting for transfers between devices  519 us (63%)
  blocking collectives  88.7 us (11%)
  starting transfers between devices  49.8 us (6%)
  local copies, waits for them, and re-layouts  45.8 us (6%)
  matrix products  41.1 us (5%)
  Pallas kernels  33.9 us (4%)
  other arithmetic  20.3 us (2%)
  between operations  16.4 us (2%)
    ppermute x10, waiting for transfers between devices, tick(): inbound = lax.ppermute(output_rows, 'section', RELAY)  405 us
    all_to_all x4, blocking collectives, mixture(): lax.all_to_all(outgoing, 'expert', split_axis=0, concat_axis=0, tiled=True)  88.7 us
    ppermute x6, waiting for transfers between devices, relocated(): return jnp.where(here, value, lax.ppermute(value, 'section', MOVES))  74.3 us
    all_to_all x4, waiting for transfers between devices, mixture(): lax.all_to_all(produced, 'expert', split_axis=0, concat_axis=0, tiled=True)  27.7 us
    pallas_call x4, Pallas kernels, expert_rows(): pl.pallas_call(expert_kernel, out_shape=[jax.ShapeDtypeStruct((count, mod...  25.6 us
    all_to_all x4, starting transfers between devices, mixture(): lax.all_to_all(produced, 'expert', split_axis=0, concat_axis=0, tiled=True)  20.1 us
  transfers between devices with their start and end apart: 22, of which 19 were waited for; matrix products, arithmetic and copies ran while one was open for 9% of the time, Pallas kernels for 0%

profile of v5, /device:TPU:13, one launch (start us, length us, event | category | flops | bytes accessed | tf_op | source)
XLA Modules:
  0.0 820.6 jit_solution(3997473787857278325)
XLA Ops:
  13.3 4.0 collective-permute-done.2
  21.7 4.2 collective-permute-start.1
  35.9 50.8 %collective-permute-done.6 = s32[4,32,12]{2,1,0:T(8,128)S(1)} collective-permute-done((s32[4,32,12]{2,1,0:T(8,128)S(1)}, s32[4,32,12]{2,1,0:T(8,128)S(1)}, u32[]{:S(2)}, u32[]{:S(2)}) %collective-permute-start.6) | collective-permute-done | bytes 6176 | tf_op jit(solution)/shard_map/ppermute | solution.py:221
  98.0 19.5 %collective-permute-done.5 = bf16[704,2048]{1,0:T(8,128)(2,1)} collective-permute-done((bf16[704,2048]{1,0:T(8,128)(2,1)}, bf16[704,2048]{1,0:T(8,128)(2,1)}, u32[]{:S(2)}, u32[]{:S(2)}) %collective-permute-start.5) | collective-permute-done | bytes 2883616 | tf_op jit(solution)/shard_map/ppermute | solution.py:221
  128.1 6.1 fusion.81
  137.4 661.9 %while.23 = (s32[]{:T(128)}, bf16[32,2048]{1,0:T(8,128)(2,1)}, bf16[128,128]{1,0:T(8,128)(2,1)}, bf16[128,128]{1,0:T(8,128)(2,1)}, bf16[11,32,2048]{2,1,0:T(8,12...) while((s32[]{:T(128)}, bf16[32,2048]{1,0:T(8,128)(2,1)}, ...), condition=%wide.region_13.14_spmd, body=%wide.region_8.13_spmd.sunk | while | flops 2609557760 | bytes 39108424 | solution.py:363
  140.8 10.7 %collective-permute-done = bf16[32,2048]{1,0:T(8,128)(2,1)S(1)} collective-permute-done((bf16[32,2048]{1,0:T(8,128)(2,1)}, bf16[32,2048]{1,0:T(8,128)(2,1)S(1)}, u32[]{:S(2)}, u32[]{:S(2)}) %collective-permute-start) | collective-permute-done | bytes 131104 | tf_op jit(solution)/shard_map/while/body/eval_jaxpr/ppermute | solution.py:359
  155.6 4.0 collective-permute-done
  179.8 4.0 collective-permute-done
  196.0 357.8 %collective-permute-done = bf16[32,2048]{1,0:T(8,128)(2,1)S(1)} collective-permute-done((bf16[32,2048]{1,0:T(8,128)(2,1)}, bf16[32,2048]{1,0:T(8,128)(2,1)S(1)}, u32[]{:S(2)}, u32[]{:S(2)}) %collective-permute-start) | collective-permute-done | bytes 131104 | tf_op jit(solution)/shard_map/while/body/eval_jaxpr/ppermute | solution.py:359
  553.8 54.7 %conditional.6 = (bf16[128,128]{1,0:T(8,128)(2,1)}, bf16[128,128]{1,0:T(8,128)(2,1)}, bf16[32,2048]{1,0:T(8,128)(2,1)}) conditional(s32[]{:T(128)} %convert_element_type.166, (bf16[128,128]{1,0:T(8,128)(2,1)}, bf16[128,128]{1,0:T(8,128)(2,1)}) %tuple.101, (s32[]{:T(128)}, s32[1]{0:T(128)}, bf16[32,2048]{1,0:T(8,128)(2,1)S(1)}, ...), branch_computations={%region_9.9_spmd, %region_10.12_spmd} | conditional | flops 2609557760 | bytes 38321084 | solution.py:352
  555.8 22.2 %all_to_all.18 = bf16[32,8,2048]{2,1,0:T(8,128)(2,1)S(1)} all-to-all(bf16[32,8,2048]{2,1,0:T(8,128)(2,1)S(1)} %bitcast.156), channel_id=1, replica_groups=mesh['section'=8,'expert'=32] {'expert'}, dimensions={0} | all-to-all | bytes 2097152 | tf_op jit(solution)/shard_map/while/body/eval_jaxpr/cond/branch_1_fun/all_to_all | solution.py:268
  578.0 6.4 experts.3
  584.4 5.0 all-to-all-start.3
  599.9 6.9 all-to-all-done.3
  615.9 54.7 %conditional.6 = (bf16[128,128]{1,0:T(8,128)(2,1)}, bf16[128,128]{1,0:T(8,128)(2,1)}, bf16[32,2048]{1,0:T(8,128)(2,1)}) conditional(s32[]{:T(128)} %convert_element_type.166, (bf16[128,128]{1,0:T(8,128)(2,1)}, bf16[128,128]{1,0:T(8,128)(2,1)}) %tuple.101, (s32[]{:T(128)}, s32[1]{0:T(128)}, bf16[32,2048]{1,0:T(8,128)(2,1)S(1)}, ...), branch_computations={%region_9.9_spmd, %region_10.12_spmd} | conditional | flops 2609557760 | bytes 38321084 | solution.py:352
  618.0 22.2 %all_to_all.18 = bf16[32,8,2048]{2,1,0:T(8,128)(2,1)S(1)} all-to-all(bf16[32,8,2048]{2,1,0:T(8,128)(2,1)S(1)} %bitcast.156), channel_id=1, replica_groups=mesh['section'=8,'expert'=32] {'expert'}, dimensions={0} | all-to-all | bytes 2097152 | tf_op jit(solution)/shard_map/while/body/eval_jaxpr/cond/branch_1_fun/all_to_all | solution.py:268
  640.2 6.4 experts.3
  646.6 5.0 all-to-all-start.3
  662.0 6.9 all-to-all-done.3
  678.1 54.7 %conditional.6 = (bf16[128,128]{1,0:T(8,128)(2,1)}, bf16[128,128]{1,0:T(8,128)(2,1)}, bf16[32,2048]{1,0:T(8,128)(2,1)}) conditional(s32[]{:T(128)} %convert_element_type.166, (bf16[128,128]{1,0:T(8,128)(2,1)}, bf16[128,128]{1,0:T(8,128)(2,1)}) %tuple.101, (s32[]{:T(128)}, s32[1]{0:T(128)}, bf16[32,2048]{1,0:T(8,128)(2,1)S(1)}, ...), branch_computations={%region_9.9_spmd, %region_10.12_spmd} | conditional | flops 2609557760 | bytes 38321084 | solution.py:352
  680.1 22.2 %all_to_all.18 = bf16[32,8,2048]{2,1,0:T(8,128)(2,1)S(1)} all-to-all(bf16[32,8,2048]{2,1,0:T(8,128)(2,1)S(1)} %bitcast.156), channel_id=1, replica_groups=mesh['section'=8,'expert'=32] {'expert'}, dimensions={0} | all-to-all | bytes 2097152 | tf_op jit(solution)/shard_map/while/body/eval_jaxpr/cond/branch_1_fun/all_to_all | solution.py:268
  702.3 6.4 experts.3
  708.7 5.0 all-to-all-start.3
  724.2 6.9 all-to-all-done.3
  736.2 8.4 %collective-permute-done = bf16[32,2048]{1,0:T(8,128)(2,1)S(1)} collective-permute-done((bf16[32,2048]{1,0:T(8,128)(2,1)}, bf16[32,2048]{1,0:T(8,128)(2,1)S(1)}, u32[]{:S(2)}, u32[]{:S(2)}) %collective-permute-start) | collective-permute-done | bytes 131104 | tf_op jit(solution)/shard_map/while/body/eval_jaxpr/ppermute | solution.py:359
  744.6 54.7 %conditional.6 = (bf16[128,128]{1,0:T(8,128)(2,1)}, bf16[128,128]{1,0:T(8,128)(2,1)}, bf16[32,2048]{1,0:T(8,128)(2,1)}) conditional(s32[]{:T(128)} %convert_element_type.166, (bf16[128,128]{1,0:T(8,128)(2,1)}, bf16[128,128]{1,0:T(8,128)(2,1)}) %tuple.101, (s32[]{:T(128)}, s32[1]{0:T(128)}, bf16[32,2048]{1,0:T(8,128)(2,1)S(1)}, ...), branch_computations={%region_9.9_spmd, %region_10.12_spmd} | conditional | flops 2609557760 | bytes 38321084 | solution.py:352
  746.7 22.2 %all_to_all.18 = bf16[32,8,2048]{2,1,0:T(8,128)(2,1)S(1)} all-to-all(bf16[32,8,2048]{2,1,0:T(8,128)(2,1)S(1)} %bitcast.156), channel_id=1, replica_groups=mesh['section'=8,'expert'=32] {'expert'}, dimensions={0} | all-to-all | bytes 2097152 | tf_op jit(solution)/shard_map/while/body/eval_jaxpr/cond/branch_1_fun/all_to_all | solution.py:268
  768.8 6.4 experts.3
  775.3 5.0 all-to-all-start.3
  790.7 6.9 all-to-all-done.3
  803.9 8.0 collective-permute-done.7
  (159 shorter events, 164.5 us)
Async XLA Ops:
  6.5 22.2 %copy-start.10 = (s32[1,4,32,6]{2,1,3,0:T(4,128)S(1)}, s32[1,4,32,6]{2,1,3,0:T(4,128)}, u32[]{:S(2)}) copy-start(s32[1,4,32,6]{2,1,3,0:T(4,128)} %param.32) | copy-start | bytes 9220
  6.5 22.2 %copy-start.11 = (s32[1,4,32,6]{2,1,3,0:T(4,128)S(1)}, s32[1,4,32,6]{2,1,3,0:T(4,128)}, u32[]{:S(2)}) copy-start(s32[1,4,32,6]{2,1,3,0:T(4,128)} %param.31) | copy-start | bytes 9220
  6.5 118.8 %all-gather.2.cloned.1.call-start = ((), (), s32[]{:S(2)}) async-start(), calls=%async_computation.4 | async-start | bytes 9732096 | tf_op jit(solution)/shard_map/all_gather | solution.py:236
  7.4 82.6 %copy-start.8 = (f32[1,2048]{1,0:T(1,128)S(1)}, f32[1,2048]{1,0:T(1,128)}, u32[]{:S(2)}) copy-start(f32[1,2048]{1,0:T(1,128)} %param.23) | copy-start | bytes 24580
  7.5 82.6 %copy-start.9 = (f32[1,2048]{1,0:T(1,128)S(1)}, f32[1,2048]{1,0:T(1,128)}, u32[]{:S(2)}) copy-start(f32[1,2048]{1,0:T(1,128)} %param.22) | copy-start | bytes 24580
  7.5 82.6 %copy-start.3 = (bf16[1,1,2048,704]{2,3,1,0:T(8,128)(2,1)S(1)}, bf16[1,1,2048,704]{2,3,1,0:T(8,128)(2,1)}, u32[]{:S(2)}) copy-start(bf16[1,1,2048,704]{2,3,1,0:T(8,128)(2,1)} %param.28) | copy-start | bytes 8650756
  9.3 8.0 collective-permute-start.2
  19.0 71.1 %collective-permute-start.3 = (bf16[704,2048]{1,0:T(8,128)(2,1)}, bf16[704,2048]{1,0:T(8,128)(2,1)}, u32[]{:S(2)}, u32[]{:S(2)}) collective-permute-start(bf16[704,2048]{1,0:T(8,128)(2,1)} %bitcast.164), channel_id=1, source_target_pairs={{32,192},{96,128},{128,224},{160,96},{192,32},{224,160},{33,193},{... | collective-permute-start | bytes 8650760 | tf_op jit(solution)/shard_map/ppermute | solution.py:221
  21.7 68.4 %collective-permute-start.1 = (f32[2,2048]{1,0:T(2,128)S(1)}, f32[2,2048]{1,0:T(2,128)S(1)}, u32[]{:S(2)}, u32[]{:S(2)}) collective-permute-start(f32[2,2048]{1,0:T(2,128)S(1)} %pad_maximum_fusion), channel_id=1, source_target_pairs={{32,192},{96,128},{128,224},{160,96},{192,32},{224,160},{33,193},{... | collective-permute-start | bytes 49160 | tf_op jit(solution)/shard_map/ppermute | solution.py:221
  25.9 68.2 %collective-permute-start.4 = (bf16[704,2048]{1,0:T(8,128)(2,1)}, bf16[704,2048]{1,0:T(8,128)(2,1)}, u32[]{:S(2)}, u32[]{:S(2)}) collective-permute-start(bf16[704,2048]{1,0:T(8,128)(2,1)} %bitcast.166), channel_id=1, source_target_pairs={{32,192},{96,128},{128,224},{160,96},{192,32},{224,160},{33,193},{... | collective-permute-start | bytes 8650760 | tf_op jit(solution)/shard_map/ppermute | solution.py:221
  28.9 57.8 %collective-permute-start.6 = (s32[4,32,12]{2,1,0:T(8,128)S(1)}, s32[4,32,12]{2,1,0:T(8,128)S(1)}, u32[]{:S(2)}, u32[]{:S(2)}) collective-permute-start(s32[4,32,12]{2,1,0:T(8,128)S(1)} %copy.41), channel_id=1, source_target_pairs={{32,192},{96,128},{128,224},{160,96},{192,32},{224,160},{33,193},{... | collective-permute-start | bytes 18440 | tf_op jit(solution)/shard_map/ppermute | solution.py:221
  34.0 83.6 %collective-permute-start.5 = (bf16[704,2048]{1,0:T(8,128)(2,1)}, bf16[704,2048]{1,0:T(8,128)(2,1)}, u32[]{:S(2)}, u32[]{:S(2)}) collective-permute-start(bf16[704,2048]{1,0:T(8,128)(2,1)} %bitcast.168), channel_id=1, source_target_pairs={{32,192},{96,128},{128,224},{160,96},{192,32},{224,160},{33,193},{... | collective-permute-start | bytes 8650760 | tf_op jit(solution)/shard_map/ppermute | solution.py:221
  90.1 3.9 copy-start.4
  94.1 23.5 %copy-start.6 = (bf16[1,1,704,2048]{3,2,1,0:T(8,128)(2,1)S(1)}, bf16[1,1,704,2048]{3,2,1,0:T(8,128)(2,1)}, u32[]{:S(2)}) copy-start(bf16[1,1,704,2048]{3,2,1,0:T(8,128)(2,1)} %param.30) | copy-start | bytes 8650756
  128.1 6.1 copy-start
  137.4 14.1 %collective-permute-start = (bf16[32,2048]{1,0:T(8,128)(2,1)}, bf16[32,2048]{1,0:T(8,128)(2,1)S(1)}, u32[]{:S(2)}, u32[]{:S(2)}) collective-permute-start(bf16[32,2048]{1,0:T(8,128)(2,1)} %get-tuple-element.878), channel_id=1, source_target_pairs={{0,192},{192,64},{64,128},{128,224},{224,96},{96,32},{32,160},{1,1... | collective-permute-start | bytes 393224 | tf_op jit(solution)/shard_map/while/body/eval_jaxpr/ppermute | solution.py:359
  152.2 7.4 collective-permute-start
  160.3 7.4 collective-permute-start
  168.3 7.4 collective-permute-start
  176.4 7.4 collective-permute-start
  184.5 7.4 collective-permute-start
  192.6 361.2 %collective-permute-start = (bf16[32,2048]{1,0:T(8,128)(2,1)}, bf16[32,2048]{1,0:T(8,128)(2,1)S(1)}, u32[]{:S(2)}, u32[]{:S(2)}) collective-permute-start(bf16[32,2048]{1,0:T(8,128)(2,1)} %get-tuple-element.878), channel_id=1, source_target_pairs={{0,192},{192,64},{64,128},{128,224},{224,96},{96,32},{32,160},{1,1... | collective-permute-start | bytes 393224 | tf_op jit(solution)/shard_map/while/body/eval_jaxpr/ppermute | solution.py:359
  584.4 22.4 %all-to-all-start.3 = ((bf16[32,8,2048]{2,1,0:T(8,128)(2,1)}), bf16[32,8,2048]{2,1,0:T(8,128)(2,1)S(1)}, u32[]{:S(2)}, u32[]{:S(2)}) async-start(bf16[32,8,2048]{2,1,0:T(8,128)(2,1)} %bitcast.19), calls=%async_computation.3 | async-start | bytes 2097152 | tf_op jit(solution)/shard_map/while/body/eval_jaxpr/cond/branch_1_fun/all_to_all | solution.py:271
  597.0 1.6 copy-start.2
  608.5 7.4 collective-permute-start
  646.6 22.4 %all-to-all-start.3 = ((bf16[32,8,2048]{2,1,0:T(8,128)(2,1)}), bf16[32,8,2048]{2,1,0:T(8,128)(2,1)S(1)}, u32[]{:S(2)}, u32[]{:S(2)}) async-start(bf16[32,8,2048]{2,1,0:T(8,128)(2,1)} %bitcast.19), calls=%async_computation.3 | async-start | bytes 2097152 | tf_op jit(solution)/shard_map/while/body/eval_jaxpr/cond/branch_1_fun/all_to_all | solution.py:271
  659.1 1.6 copy-start.2
  670.6 7.4 collective-permute-start
  708.7 22.4 %all-to-all-start.3 = ((bf16[32,8,2048]{2,1,0:T(8,128)(2,1)}), bf16[32,8,2048]{2,1,0:T(8,128)(2,1)S(1)}, u32[]{:S(2)}, u32[]{:S(2)}) async-start(bf16[32,8,2048]{2,1,0:T(8,128)(2,1)} %bitcast.19), calls=%async_computation.3 | async-start | bytes 2097152 | tf_op jit(solution)/shard_map/while/body/eval_jaxpr/cond/branch_1_fun/all_to_all | solution.py:271
  732.8 11.8 %collective-permute-start = (bf16[32,2048]{1,0:T(8,128)(2,1)}, bf16[32,2048]{1,0:T(8,128)(2,1)S(1)}, u32[]{:S(2)}, u32[]{:S(2)}) collective-permute-start(bf16[32,2048]{1,0:T(8,128)(2,1)} %get-tuple-element.878), channel_id=1, source_target_pairs={{0,192},{192,64},{64,128},{128,224},{224,96},{96,32},{32,160},{1,1... | collective-permute-start | bytes 393224 | tf_op jit(solution)/shard_map/while/body/eval_jaxpr/ppermute | solution.py:359
  775.3 22.4 %all-to-all-start.3 = ((bf16[32,8,2048]{2,1,0:T(8,128)(2,1)}), bf16[32,8,2048]{2,1,0:T(8,128)(2,1)S(1)}, u32[]{:S(2)}, u32[]{:S(2)}) async-start(bf16[32,8,2048]{2,1,0:T(8,128)(2,1)} %bitcast.19), calls=%async_computation.3 | async-start | bytes 2097152 | tf_op jit(solution)/shard_map/while/body/eval_jaxpr/cond/branch_1_fun/all_to_all | solution.py:271
  802.0 9.9 %collective-permute-start.7 = (bf16[4,32,2048]{2,1,0:T(8,128)(2,1)S(1)}, bf16[4,32,2048]{2,1,0:T(8,128)(2,1)S(1)}, u32[]{:S(2)}, u32[]{:S(2)}) collective-permute-start(bf16[4,32,2048]{2,1,0:T(8,128)(2,1)S(1)} %constant_dynamic-slice_fusion), channel_id=1, source_target_pairs={{192,32},{128,96},{224,128},{96,160},{32,192},{160,224},{193,33},{... | collective-permute-start | bytes 1572872 | tf_op jit(solution)/shard_map/ppermute | solution.py:366
  (6 other events, 5.8 us)
Sparse Core Ops, SparseCore 0:
  19.1 106.1 all-gather.1
